TPU v7x, 8 devices: a whole 2x2x1 slice. The times are simulated.
8 devices in a mesh: mp: 1 (over z), dpa: 2 (over y), dpb: 2 (over x), dpc: 2 (over core).
Axes of the slice: x: 2, y: 2, z: 1, core: 2. Of those that a mesh axis runs over, the one named last changes fastest.
Arguments:
- x: bfloat16 [65536, 768], P(('mp', 'dpa', 'dpb', 'dpc'))
- g: bfloat16 [65536, 768], P(('mp', 'dpa', 'dpb', 'dpc'))
- w1: bfloat16 [768, 3072], P('mp')
- w2: bfloat16 [3072, 768], P('mp')
- w3: bfloat16 [768, 3072], P('mp')
- w4: bfloat16 [3072, 768], P('mp')
Outputs:
- output 1: float32 [768, 3072], P('mp')
- output 2: float32 [3072, 768], P('mp')
- output 3: float32 [768, 3072], P('mp')
- output 4: float32 [3072, 768], P('mp')
- output 5: bfloat16 [65536, 768], P(('mp', 'dpa', 'dpb', 'dpc'))
All inputs are finite; a program needn't handle non-finite values.
Results may differ from a plain program's by a relative error of at most 0.0114143.
Values are sent between devices in bfloat16 or wider.
A program may use at most 1 GiB of HBM per device.

v0:
```python
import jax
import jax.numpy as jnp
from jax import lax
from jax.sharding import PartitionSpec as P


def gelu_grad(a, d):
    return jax.vjp(lambda t: jax.nn.gelu(t, approximate=True), a)[1](d)[0]


def solution(mesh):
    ndev = mesh.shape["dpa"] * mesh.shape["dpb"] * mesh.shape["dpc"]
    f32 = jnp.float32
    bf = jnp.bfloat16
    rows = P(("mp", "dpa", "dpb", "dpc"), None)
    wspec = P("mp", None)

    def reduce_grad(dw):
        s = lax.psum_scatter(dw, "dpc", scatter_dimension=0, tiled=True)
        s = lax.psum(s, ("dpa", "dpb"))
        return lax.all_gather(s, "dpc", axis=0, tiled=True) / ndev

    def local(x, g, w1, w2, w3, w4):
        a1 = jnp.dot(x, w1, preferred_element_type=f32).astype(bf)
        h1 = jax.nn.gelu(a1.astype(f32), approximate=True).astype(bf)
        h2 = (jnp.dot(h1, w2, preferred_element_type=f32) + x.astype(f32)).astype(bf)
        a3 = jnp.dot(h2, w3, preferred_element_type=f32).astype(bf)
        h3 = jax.nn.gelu(a3.astype(f32), approximate=True).astype(bf)
        dw4 = reduce_grad(jnp.dot(h3.T, g, preferred_element_type=f32))
        dh3 = jnp.dot(g, w4.T, preferred_element_type=f32).astype(bf)
        da3 = gelu_grad(a3.astype(f32), dh3.astype(f32)).astype(bf)
        dw3 = reduce_grad(jnp.dot(h2.T, da3, preferred_element_type=f32))
        dh2 = (jnp.dot(da3, w3.T, preferred_element_type=f32) + g.astype(f32)).astype(bf)
        dw2 = reduce_grad(jnp.dot(h1.T, dh2, preferred_element_type=f32))
        dh1 = jnp.dot(dh2, w2.T, preferred_element_type=f32).astype(bf)
        da1 = gelu_grad(a1.astype(f32), dh1.astype(f32)).astype(bf)
        dw1 = reduce_grad(jnp.dot(x.T, da1, preferred_element_type=f32))
        dx = (jnp.dot(da1, w1.T, preferred_element_type=f32) + dh2.astype(f32)).astype(bf)
        return dw1, dw2, dw3, dw4, dx

    return jax.shard_map(local, mesh=mesh, in_specs=(rows, rows, wspec, wspec, wspec, wspec), out_specs=(wspec, wspec, wspec, wspec, rows), check_vma=False)
```

profile of v0, /device:TPU:0, one launch (start us, length us, event | category | flops | bytes accessed | tf_op | source)
XLA Modules:
  0.0 1100.0 jit_solution(9972123991901462319)
XLA Ops:
  7.2 0.0 reduce-scatter.9.cloned.1.call-start
  7.2 0.0 copy-start.1
  7.2 47.3 %convolution_convert_fusion.1 = bf16[8192,3072]{1,0:T(8,128)(2,1)} fusion(bf16[8192,768]{1,0:T(8,128)(2,1)} %param.6, bf16[768,3072]{1,0:T(8,128)(2,1)} %param.8), kind=kOutput, calls=%fused_computation.36 | convolution fusion | flops 38679871488 | bytes 67633152 | tf_op jit(solution)/shard_map/dot_general | solution.py:24
  54.5 0.0 copy-done.1
  54.5 69.6 %add_convert_fusion.2 = bf16[8192,768]{1,0:T(8,128)(2,1)} fusion(bf16[8192,768]{1,0:T(8,128)(2,1)} %param.6, bf16[3072,768]{1,0:T(8,128)(2,1)S(1)} %copy-done.1, bf16[8192,3072]{1,0:T(8,128)(2,1)} %convolution_convert_fusion.1), kind=kOutput, calls=%fused_computation.39 | convolution fusion | flops 38925238272 | bytes 80216064 | tf_op jit(solution)/shard_map/dot_general | solution.py:26
  124.1 0.0 copy-start
  124.1 47.9 %convolution_convert_fusion = bf16[8192,3072]{1,0:T(8,128)(2,1)} fusion(bf16[8192,768]{1,0:T(8,128)(2,1)} %add_convert_fusion.2, bf16[768,3072]{1,0:T(8,128)(2,1)} %param.10), kind=kOutput, calls=%fused_computation.35 | convolution fusion | flops 38679871488 | bytes 67633152 | tf_op jit(solution)/shard_map/dot_general | solution.py:27
  172.0 0.0 copy-done
  172.0 98.8 %fusion.4 = bf16[8192,3072]{1,0:T(8,128)(2,1)} fusion(bf16[8192,3072]{1,0:T(8,128)(2,1)} %convolution_convert_fusion, bf16[8192,768]{1,0:T(8,128)(2,1)} %param.7, bf16[3072,768]{1,0:T(8,128)(2,1)S(1)} %copy-done), kind=kOutput, calls=%fused_computation.16 | convolution fusion | flops 39233519616 | bytes 117964800 | tf_op jit(solution)/shard_map/dot_general | solution.py:30
  270.8 48.7 %fusion.31 = f32[768,3072]{0,1:T(8,128)} fusion(bf16[8192,768]{1,0:T(8,128)(2,1)} %add_convert_fusion.2, bf16[8192,3072]{1,0:T(8,128)(2,1)} %fusion.4), kind=kOutput, calls=%fused_computation.50 | convolution fusion | flops 38654705664 | bytes 72351744 | tf_op jit(solution)/shard_map/dot_general | solution.py:32
  319.5 0.0 reduce-scatter.9.cloned.1.call-update
  319.5 0.0 reduce-scatter.11.cloned.1.call-start
  319.6 62.9 %fusion.22 = f32[3072,768]{1,0:T(8,128)} fusion(bf16[8192,768]{1,0:T(8,128)(2,1)} %param.7, bf16[8192,3072]{1,0:T(8,128)(2,1)} %convolution_convert_fusion), kind=kOutput, calls=%fused_computation.34 | convolution fusion | flops 38906363904 | bytes 72351744 | tf_op jit(solution)/shard_map/dot_general | solution.py:29
  382.5 0.0 reduce-scatter.11.cloned.1.call-update
  382.6 0.0 reduce-scatter.5.cloned.1.call-start
  382.6 0.0 copy-start.2
  382.6 47.6 %add_convert_fusion.1 = bf16[8192,768]{1,0:T(8,128)(2,1)} fusion(bf16[8192,768]{1,0:T(8,128)(2,1)} %param.7, bf16[8192,3072]{1,0:T(8,128)(2,1)} %fusion.4, bf16[768,3072]{1,0:T(8,128)(2,1)} %param.10), kind=kOutput, calls=%fused_computation.38 | convolution fusion | flops 38673580032 | bytes 80216064 | tf_op jit(solution)/shard_map/dot_general | solution.py:33
  430.2 0.0 copy-done.2
  430.2 98.6 %fusion.7 = bf16[8192,3072]{1,0:T(8,128)(2,1)} fusion(bf16[8192,3072]{1,0:T(8,128)(2,1)} %convolution_convert_fusion.1, bf16[8192,768]{1,0:T(8,128)(2,1)} %add_convert_fusion.1, bf16[3072,768]{1,0:T(8,128)(2,1)S(1)} %copy-done.2), kind=kOutput, calls=%fused_computation.19 | convolution fusion | flops 39233519616 | bytes 117964800 | tf_op jit(solution)/shard_map/dot_general | solution.py:35
  528.9 48.6 %convolution_bitcast_fusion = f32[768,3072]{0,1:T(8,128)} fusion(bf16[8192,3072]{1,0:T(8,128)(2,1)} %fusion.7, bf16[8192,768]{1,0:T(8,128)(2,1)} %param.6), kind=kOutput, calls=%fused_computation.40 | convolution fusion | flops 38654705664 | bytes 72351744 | tf_op jit(solution)/shard_map/dot_general | solution.py:37
  577.5 0.0 reduce-scatter.5.cloned.1.call-update
  577.5 0.0 reduce-scatter.7.cloned.1.call-start
  577.6 62.9 %fusion.28 = f32[3072,768]{1,0:T(8,128)} fusion(bf16[8192,768]{1,0:T(8,128)(2,1)} %add_convert_fusion.1, bf16[8192,3072]{1,0:T(8,128)(2,1)} %convolution_convert_fusion.1), kind=kOutput, calls=%fused_computation.49 | convolution fusion | flops 38906363904 | bytes 72351744 | tf_op jit(solution)/shard_map/dot_general | solution.py:34
  640.5 0.0 reduce-scatter.7.cloned.1.call-update
  640.5 0.0 all-reduce.3.cloned.1.call-start
  640.5 0.0 reduce-scatter.9.cloned.1.call-done
  640.6 0.0 reduce-scatter.11.cloned.1.call-done
  640.6 0.0 reduce-scatter.5.cloned.1.call-done
  640.6 16.7 %reduce-scatter.7.cloned.1.call-done = f32[1536,768]{1,0:T(8,128)} async-done(((f32[3072,768]{1,0:T(8,128)}), f32[1536,768]{1,0:T(8,128)}) %reduce-scatter.7.cloned.1.call-update) | async-done | bytes 4718608 | tf_op jit(solution)/shard_map/reduce_scatter | solution.py:19
  657.3 0.0 all-reduce.3.cloned.1.call-update
  657.4 0.0 all-gather.5.cloned.1.call-start
  657.4 334.9 %all-reduce.3.cloned.1.call-done = (f32[384,3072]{0,1:T(8,128)}, f32[1536,768]{1,0:T(8,128)}, f32[384,3072]{0,1:T(8,128)}, f32[1536,768]{1,0:T(8,128)}) async-done(((f32[384,3072]{0,1:T(8,128)}, f32[1536,768]{1,0:T(8,128)}, f32[384,3072]{0,1:T(8,128)}, f32[1536,768]{1,0:T(8,128)}), (f32[384,3072]{0,1:T(8,128)}, f32[1536,768]{1,0:T(8,128)}, f32[384,3072]{0,1:T(8,128)}, ...) | async-done | bytes 18874384 | tf_op jit(solution)/shard_map/psum | solution.py:20
  992.3 0.0 all-gather.5.cloned.1.call-update
  992.3 0.0 all-gather.9.cloned.1.call-start
  992.4 0.7 all-gather.9.cloned.1.call-update
  993.1 0.0 all-gather.7.cloned.1.call-start
  993.1 0.7 all-gather.7.cloned.1.call-update
  993.8 0.0 all-gather.11.cloned.1.call-start
  993.9 0.7 all-gather.11.cloned.1.call-update
  994.5 47.5 %add_convert_fusion = bf16[8192,768]{1,0:T(8,128)(2,1)} fusion(bf16[8192,768]{1,0:T(8,128)(2,1)} %add_convert_fusion.1, bf16[8192,3072]{1,0:T(8,128)(2,1)} %fusion.7, bf16[768,3072]{1,0:T(8,128)(2,1)} %param.8), kind=kOutput, calls=%fused_computation.37 | convolution fusion | flops 38673580032 | bytes 80216064 | tf_op jit(solution)/shard_map/dot_general | solution.py:38
  1042.0 0.0 all-gather.5.cloned.1.call-done
  1042.0 8.0 broadcast_multiply_fusion.3
  1050.0 9.6 copy.12
  1059.6 0.0 all-gather.9.cloned.1.call-done
  1059.6 8.0 broadcast_multiply_fusion.2
  1067.6 9.6 copy.13
  1077.2 0.0 all-gather.7.cloned.1.call-done
  1077.2 8.0 broadcast_multiply_fusion.1
  1085.3 0.0 all-gather.11.cloned.1.call-done
  1085.3 8.0 broadcast_multiply_fusion
Async XLA Ops:
  7.2 633.4 %reduce-scatter.9.cloned.1.call-start = ((), (), s32[]{:S(2)}) async-start(), calls=%async_computation.8 | async-start | bytes 14155776 | tf_op jit(solution)/shard_map/reduce_scatter | solution.py:19
  7.2 47.3 %copy-start.1 = (bf16[3072,768]{1,0:T(8,128)(2,1)S(1)}, bf16[3072,768]{1,0:T(8,128)(2,1)}, u32[]{:S(2)}) copy-start(bf16[3072,768]{1,0:T(8,128)(2,1)} %param.9) | copy-start | bytes 14155780
  124.1 47.9 %copy-start = (bf16[3072,768]{1,0:T(8,128)(2,1)S(1)}, bf16[3072,768]{1,0:T(8,128)(2,1)}, u32[]{:S(2)}) copy-start(bf16[3072,768]{1,0:T(8,128)(2,1)} %param.11) | copy-start | bytes 14155780
  319.5 321.0 %reduce-scatter.11.cloned.1.call-start = ((), (), s32[]{:S(2)}) async-start(), calls=%async_computation.10 | async-start | bytes 14155776 | tf_op jit(solution)/shard_map/reduce_scatter | solution.py:19
  382.6 258.0 %reduce-scatter.5.cloned.1.call-start = ((), (), s32[]{:S(2)}) async-start(), calls=%async_computation.4 | async-start | bytes 14155776 | tf_op jit(solution)/shard_map/reduce_scatter | solution.py:19
  382.6 47.6 %copy-start.2 = (bf16[3072,768]{1,0:T(8,128)(2,1)S(1)}, bf16[3072,768]{1,0:T(8,128)(2,1)}, u32[]{:S(2)}) copy-start(bf16[3072,768]{1,0:T(8,128)(2,1)} %param.9) | copy-start | bytes 14155780
  577.5 79.8 %reduce-scatter.7.cloned.1.call-start = ((), (), s32[]{:S(2)}) async-start(), calls=%async_computation.6 | async-start | bytes 14155776 | tf_op jit(solution)/shard_map/reduce_scatter | solution.py:19
  640.5 351.8 %all-reduce.3.cloned.1.call-start = ((), (), s32[]{:S(2)}) async-start(), calls=%async_computation.12 | async-start | bytes 37748736 | tf_op jit(solution)/shard_map/psum | solution.py:20
  657.4 384.6 %all-gather.5.cloned.1.call-start = ((), (), s32[]{:S(2)}) async-start(), calls=%async_computation.5 | async-start | bytes 14155776 | tf_op jit(solution)/shard_map/all_gather | solution.py:21
  992.3 67.3 %all-gather.9.cloned.1.call-start = ((), (), s32[]{:S(2)}) async-start(), calls=%async_computation.9 | async-start | bytes 14155776 | tf_op jit(solution)/shard_map/all_gather | solution.py:21
  993.1 84.2 %all-gather.7.cloned.1.call-start = ((), (), s32[]{:S(2)}) async-start(), calls=%async_computation.7 | async-start | bytes 14155776 | tf_op jit(solution)/shard_map/all_gather | solution.py:21
  993.8 91.4 %all-gather.11.cloned.1.call-start = ((), (), s32[]{:S(2)}) async-start(), calls=%async_computation.11 | async-start | bytes 14155776 | tf_op jit(solution)/shard_map/all_gather | solution.py:21
Sparse Core Ops, SparseCore 0:
  319.7 16.6 reduce-scatter.8
  382.7 16.6 reduce-scatter.10
  577.7 16.6 reduce-scatter.4
  640.6 16.6 reduce-scatter.6
  661.1 331.1 all-reduce.2
  993.7 21.1 all-gather.4
  1016.4 20.9 all-gather.8
  1039.0 20.9 all-gather.6
  1061.5 20.9 all-gather.10
where the time goes:
time: 1110 us; the launch traced here: 1100 us
  matrix products  680 us (61%)
  waiting for transfers between devices  354 us (32%)
  other arithmetic  32.1 us (3%)
  local copies, waits for them, and re-layouts  19.2 us (2%)
  between operations  14.1 us (1%)
    psum x1, waiting for transfers between devices, reduce_grad(): s = lax.psum(s, ('dpa', 'dpb'))  335 us
    dot_general x1, matrix products, local(): dh3 = jnp.dot(g, w4.T, preferred_element_type=f32).astype(bf)  98.8 us
    dot_general x1, matrix products, local(): dh1 = jnp.dot(dh2, w2.T, preferred_element_type=f32).astype(bf)  98.6 us
    dot_general x1, matrix products, local(): jnp.dot(h1, w2, preferred_element_type=f32) + x.astype(f32)  69.6 us
    dot_general x1, matrix products, local(): dw4 = reduce_grad(jnp.dot(h3.T, g, preferred_element_type=f32))  62.9 us
    dot_general x1, matrix products, local(): dw2 = reduce_grad(jnp.dot(h1.T, dh2, preferred_element_type=f32))  62.9 us
    dot_general x1, matrix products, local(): dw3 = reduce_grad(jnp.dot(h2.T, da3, preferred_element_type=f32))  48.7 us
    dot_general x1, matrix products, local(): dw1 = reduce_grad(jnp.dot(x.T, da1, preferred_element_type=f32))  48.6 us
  transfers between devices with their start and end apart: 9, of which 2 were waited for; matrix products, arithmetic and copies ran while one was open for 37% of the time, Pallas kernels for 0%

commit v1 on v0

v1 whole, which is shorter than its diff:
```python
import functools
import jax, jax.numpy as jnp
from jax import lax
from jax.experimental import pallas as pl
from jax.experimental.pallas import tpu as pltpu
from jax.sharding import PartitionSpec as P
f32=jnp.float32; bf=jnp.bfloat16
D=768; F=3072; N=8192
C1=0.7978845608028654; C2=C1*0.044715
def nn(a,b): return lax.dot_general(a,b,(((1,),(0,)),((),())),preferred_element_type=f32)
def nt(a,b): return lax.dot_general(a,b,(((1,),(1,)),((),())),preferred_element_type=f32)
def tn(a,b): return lax.dot_general(a,b,(((0,),(0,)),((),())),preferred_element_type=f32)
def gelu_f(x):
    t=jnp.tanh(x*(C1+C2*(x*x)))
    return (0.5*x)*(1.0+t)
def gelu_both(x,d):
    x2=x*x
    t=jnp.tanh(x*(C1+C2*x2))
    s=1.0+t; hx=0.5*x
    w=((1.0-t)*s)*hx
    gp=0.5*s+w*(C1+(3.0*C2)*x2)
    return hx*s, gp*d
def k1(x_ref,w1_ref,w2_ref,a1_ref,h2_ref,h1_scr,*,sub,fch):
    R=x_ref.shape[0]
    for j in range(R//sub):
        sl=pl.ds(j*sub,sub)
        for f in range(F//fch):
            fs=pl.ds(f*fch,fch)
            a1_ref[sl,fs]=nn(x_ref[sl,:],w1_ref[:,fs]).astype(bf)
            h1_scr[sl,fs]=gelu_f(a1_ref[sl,fs].astype(f32)).astype(bf)
        h2_ref[sl,:]=(nn(h1_scr[sl,:],w2_ref[...])+x_ref[sl,:].astype(f32)).astype(bf)
def call_k1(x,w1,w2,R=512,sub=256,fch=768):
    return pl.pallas_call(functools.partial(k1,sub=sub,fch=fch),grid=(N//R,),
      in_specs=[pl.BlockSpec((R,D),lambda r:(r,0)),pl.BlockSpec((D,F),lambda r:(0,0)),pl.BlockSpec((F,D),lambda r:(0,0))],
      out_specs=[pl.BlockSpec((R,F),lambda r:(r,0)),pl.BlockSpec((R,D),lambda r:(r,0))],
      out_shape=[jax.ShapeDtypeStruct((N,F),bf),jax.ShapeDtypeStruct((N,D),bf)],
      scratch_shapes=[pltpu.VMEM((R,F),bf)],
      compiler_params=pltpu.CompilerParams(vmem_limit_bytes=60*2**20),name="k1",cost_estimate=pl.CostEstimate(flops=4*N*D*F,bytes_accessed=2*N*(F+2*D),transcendentals=N*F))(x,w1,w2)
def k2(h2_ref,g_ref,w3_ref,w4_ref,da3_ref,p3_ref,p4_ref,a_scr,d_scr,h_scr,*,sub):
    R=h2_ref.shape[0]; n=R//sub
    r=pl.program_id(1)
    @pl.when(r==0)
    def _():
        p3_ref[...]=jnp.zeros_like(p3_ref); p4_ref[...]=jnp.zeros_like(p4_ref)
    def dd(j):
        sl=pl.ds(j*sub,sub)
        a_scr[sl,:]=nn(h2_ref[sl,:],w3_ref[...]).astype(bf)
        d_scr[sl,:]=nt(g_ref[sl,:],w4_ref[...]).astype(bf)
    def ee(j):
        sl=pl.ds(j*sub,sub)
        h,da=gelu_both(a_scr[sl,:].astype(f32),d_scr[sl,:].astype(f32))
        h_scr[sl,:]=h.astype(bf); da3_ref[sl,:]=da.astype(bf)
    def pp(j):
        sl=pl.ds(j*sub,sub)
        p4_ref[...]+=tn(h_scr[sl,:],g_ref[sl,:])
        p3_ref[...]+=tn(h2_ref[sl,:],da3_ref[sl,:])
    for j in range(n):
        dd(j)
        if j>0: ee(j-1)
        if j>1: pp(j-2)
    ee(n-1)
    if n>1: pp(n-2)
    pp(n-1)
def call_k2(h2,g,w3,w4,R=1024,sub=512,fc=768):
    return pl.pallas_call(functools.partial(k2,sub=sub),grid=(F//fc,N//R),
      in_specs=[pl.BlockSpec((R,D),lambda c,r:(r,0)),pl.BlockSpec((R,D),lambda c,r:(r,0)),pl.BlockSpec((D,fc),lambda c,r:(0,c)),pl.BlockSpec((fc,D),lambda c,r:(c,0))],
      out_specs=[pl.BlockSpec((R,fc),lambda c,r:(r,c)),pl.BlockSpec((D,fc),lambda c,r:(0,c)),pl.BlockSpec((fc,D),lambda c,r:(c,0))],
      out_shape=[jax.ShapeDtypeStruct((N,F),bf),jax.ShapeDtypeStruct((D,F),f32),jax.ShapeDtypeStruct((F,D),f32)],
      scratch_shapes=[pltpu.VMEM((R,fc),bf)]*3,
      compiler_params=pltpu.CompilerParams(vmem_limit_bytes=60*2**20),name="k2",cost_estimate=pl.CostEstimate(flops=8*N*D*F,bytes_accessed=2*N*(F+8*D),transcendentals=N*F))(h2,g,w3,w4)
def k3(*refs,sub):
    *a_refs,w_ref,r_ref,o_ref=refs
    R=r_ref.shape[0]
    for j in range(R//sub):
        sl=pl.ds(j*sub,sub)
        acc=r_ref[sl,:].astype(f32)
        k=0
        for a_ref in a_refs:
            w=a_ref.shape[1]
            acc=nt(a_ref[sl,:],w_ref[:,k:k+w])+acc
            k+=w
        o_ref[sl,:]=acc.astype(bf)
def call_k3(parts,w,res,R=1024,sub=512):
    return pl.pallas_call(functools.partial(k3,sub=sub),grid=(N//R,),
      in_specs=[pl.BlockSpec((R,a.shape[1]),lambda r:(r,0)) for a in parts]+[pl.BlockSpec((D,F),lambda r:(0,0)),pl.BlockSpec((R,D),lambda r:(r,0))],
      out_specs=pl.BlockSpec((R,D),lambda r:(r,0)),out_shape=jax.ShapeDtypeStruct((N,D),bf),
      compiler_params=pltpu.CompilerParams(vmem_limit_bytes=60*2**20),name="k3",cost_estimate=pl.CostEstimate(flops=2*N*D*F,bytes_accessed=2*N*(F+2*D),transcendentals=0))(*parts,w,res)
def k4(x_ref,dh2_ref,a1_ref,w2_ref,da1_ref,p1_ref,p2_ref,d_scr,h_scr,*,sub):
    R=x_ref.shape[0]; n=R//sub
    r=pl.program_id(1)
    @pl.when(r==0)
    def _():
        p1_ref[...]=jnp.zeros_like(p1_ref); p2_ref[...]=jnp.zeros_like(p2_ref)
    def dd(j):
        sl=pl.ds(j*sub,sub)
        d_scr[sl,:]=nt(dh2_ref[sl,:],w2_ref[...]).astype(bf)
    def ee(j):
        sl=pl.ds(j*sub,sub)
        h,da=gelu_both(a1_ref[sl,:].astype(f32),d_scr[sl,:].astype(f32))
        h_scr[sl,:]=h.astype(bf); da1_ref[sl,:]=da.astype(bf)
    def pp(j):
        sl=pl.ds(j*sub,sub)
        p2_ref[...]+=tn(h_scr[sl,:],dh2_ref[sl,:])
        p1_ref[...]+=tn(x_ref[sl,:],da1_ref[sl,:])
    for j in range(n):
        dd(j)
        if j>0: ee(j-1)
        if j>1: pp(j-2)
    ee(n-1)
    if n>1: pp(n-2)
    pp(n-1)
def call_k4(x,dh2,a1,w2,c0,nc,R=1024,sub=512,fc=768):
    return pl.pallas_call(functools.partial(k4,sub=sub),grid=(nc,N//R),
      in_specs=[pl.BlockSpec((R,D),lambda c,r:(r,0)),pl.BlockSpec((R,D),lambda c,r:(r,0)),pl.BlockSpec((R,fc),lambda c,r:(r,c+c0)),pl.BlockSpec((fc,D),lambda c,r:(c+c0,0))],
      out_specs=[pl.BlockSpec((R,fc),lambda c,r:(r,c)),pl.BlockSpec((D,fc),lambda c,r:(0,c)),pl.BlockSpec((fc,D),lambda c,r:(c,0))],
      out_shape=[jax.ShapeDtypeStruct((N,nc*fc),bf),jax.ShapeDtypeStruct((D,nc*fc),f32),jax.ShapeDtypeStruct((nc*fc,D),f32)],
      scratch_shapes=[pltpu.VMEM((R,fc),bf)]*2,
      compiler_params=pltpu.CompilerParams(vmem_limit_bytes=60*2**20),name="k4",cost_estimate=pl.CostEstimate(flops=3*N*D*F,bytes_accessed=2*N*(2*F+8*D),transcendentals=N*F))(x,dh2,a1,w2)


def solution(mesh):
    ndev = mesh.shape["dpa"] * mesh.shape["dpb"] * mesh.shape["dpc"]
    rows = P(("mp", "dpa", "dpb", "dpc"), None)
    wspec = P("mp", None)
    group = ("dpa", "dpb", "dpc")

    def scatter(dw):
        return lax.psum_scatter(dw, group, scatter_dimension=0, tiled=True)

    def gather(s):
        return lax.all_gather(s, group, axis=0, tiled=True) / ndev

    def local(x, g, w1, w2, w3, w4):
        a1, h2 = call_k1(x, w1, w2, 512, 256)
        da3, p3, p4 = call_k2(h2, g, w3, w4, 1024, 256)
        s3, s4 = scatter(p3), scatter(p4)
        dh2 = call_k3([da3], w3, g, 1024, 512)
        da1a, p1a, p2a = call_k4(x, dh2, a1, w2, 0, 2)
        da1a, dh2b, s3, s4 = lax.optimization_barrier((da1a, dh2, s3, s4))
        dw3, dw4 = gather(s3), gather(s4)
        da1b, p1b, p2b = call_k4(x, dh2b, a1, w2, 2, 2)
        s1a, s2a, s1b, s2b = scatter(p1a), scatter(p2a), scatter(p1b), scatter(p2b)
        dx = call_k3([da1a, da1b], w1, dh2, 1024, 512)
        dw1 = jnp.concatenate([gather(s1a), gather(s1b)], axis=1)
        dw2 = jnp.concatenate([gather(s2a), gather(s2b)], axis=0)
        return dw1, dw2, dw3, dw4, dx

    return jax.shard_map(local, mesh=mesh, in_specs=(rows, rows, wspec, wspec, wspec, wspec), out_specs=(wspec, wspec, wspec, wspec, rows), check_vma=False)
```

time: 1110 us -> 890 us (0.80)
  matrix products: 680 us -> 0 us
  Pallas kernels: 0 us -> 535 us
  waiting for transfers between devices: 354 us -> 296 us
  local copies, waits for them, and re-layouts: 19.2 us -> 1.73 us
    dot_general x11 -> x0, matrix products: 680 us -> none  [the longest x1 98.8 us: local(): dh3 = jnp.dot(g, w4.T, preferred_element_type=f32).astype(bf)]
    pallas_call x0 -> x6, Pallas kernels: none -> 535 us  [the longest x1 192 us: call_k2(): pl.pallas_call(functools.partial(k2, sub=sub), grid=(F // fc, N // R), in...]
    psum x1 -> x0, waiting for transfers between devices: 335 us -> none  [reduce_grad(): s = lax.psum(s, ('dpa', 'dpb'))]
    all_gather x4 -> x6, waiting for transfers between devices: 0.01 us -> 163 us  [gather(): return lax.all_gather(s, group, axis=0, tiled=True) / ndev]
    reduce_scatter x4 -> x6, waiting for transfers between devices: 16.8 us -> 129 us  [scatter(): return lax.psum_scatter(dw, group, scatter_dimension=0, tiled=True)]
    unnamed x8 -> x4, local copies, waits for them, and re-layouts: 19.2 us -> 1.73 us
    div x4 -> x6, other arithmetic: 32.1 us -> 32.7 us  [gather(): return lax.all_gather(s, group, axis=0, tiled=True) / ndev]
  transfers between devices with their start and end apart: 9 -> 12, of which waited for: 2 -> 9; matrix products, arithmetic and copies ran while one was open for 37% -> 4% of each run, Pallas kernels for 0% -> 28%
where the time goes in v1:
time: 890 us
  Pallas kernels  535 us (60%)
  waiting for transfers between devices  296 us (33%)
  other arithmetic  41.7 us (5%)
  between operations  14.2 us (2%)
    pallas_call x1, Pallas kernels, call_k2(): pl.pallas_call(functools.partial(k2, sub=sub), grid=(F // fc, N // R), in...  192 us
    all_gather x6, waiting for transfers between devices, gather(): return lax.all_gather(s, group, axis=0, tiled=True) / ndev  163 us
    pallas_call x2, Pallas kernels, call_k4(): pl.pallas_call(functools.partial(k4, sub=sub), grid=(nc, N // R), in_spec...  157 us
    reduce_scatter x6, waiting for transfers between devices, scatter(): return lax.psum_scatter(dw, group, scatter_dimension=0, tiled=True)  129 us
    pallas_call x2, Pallas kernels, call_k3(): pl.pallas_call(functools.partial(k3, sub=sub), grid=(N // R,), in_specs=[...  96.6 us
    pallas_call x1, Pallas kernels, call_k1(): pl.pallas_call(functools.partial(k1, sub=sub, fch=fch), grid=(N // R,), i...  89.6 us
    div x6, other arithmetic, gather(): return lax.all_gather(s, group, axis=0, tiled=True) / ndev  32.7 us
  transfers between devices with their start and end apart: 12, of which 9 were waited for; matrix products, arithmetic and copies ran while one was open for 4% of the time, Pallas kernels for 28%

profile of v1, /device:TPU:0, one launch (start us, length us, event | category | flops | bytes accessed | tf_op | source)
XLA Modules:
  0.0 890.0 jit_solution(7651396513238153653)
XLA Ops:
  7.2 0.0 reduce-scatter.9.cloned.1.call-start
  7.2 89.6 %k1.1 = (bf16[8192,3072]{1,0:T(8,128)(2,1)}, bf16[8192,768]{1,0:T(8,128)(2,1)}) custom-call(bf16[8192,768]{1,0:T(8,128)(2,1)} %x_ref.5, bf16[768,3072]{1,0:T(8,128)(2,1)} %refs_2_.3, bf16[3072,768]{1,0:T(8,128)(2,1)} %w2_ref.5), custom_call_target="tpu_custom_call" | custom-call | flops 77309411328 | bytes 75497472 | tf_op jit(solution)/shard_map/k1/pallas_call | solution.py:33
  96.8 192.4 %k2.1 = (bf16[8192,3072]{1,0:T(8,128)(2,1)}, f32[768,3072]{1,0:T(8,128)}, f32[3072,768]{1,0:T(8,128)}) custom-call(bf16[8192,768]{1,0:T(8,128)(2,1)} %get-tuple-element.20.h2_ref, bf16[8192,768]{1,0:T(8,128)(2,1)} %refs_2_.2, bf16[768,3072]{1,0:T(8,128)(2,1)} %refs_1_.1, bf16[3072,768]{1,0:T(8,128)(2,1)} %w4_ref.1), custom_call_target="tpu_custom_call" | custom-call | flops 154618822656 | bytes 150994944 | tf_op jit(solution)/shard_map/k2/pallas_call | solution.py:65
  289.2 0.0 reduce-scatter.9.cloned.1.call-update
  289.2 0.0 reduce-scatter.11.cloned.1.call-start
  289.3 0.7 reduce-scatter.11.cloned.1.call-update
  290.0 0.2 reduce-scatter.7.cloned.1.call-start
  290.2 48.2 %k3.2.dh2_ref.refs_3_ = bf16[8192,768]{1,0:T(8,128)(2,1)} custom-call(bf16[8192,3072]{1,0:T(8,128)(2,1)} %get-tuple-element.21.refs_0_, bf16[768,3072]{1,0:T(8,128)(2,1)} %refs_1_.1, bf16[8192,768]{1,0:T(8,128)(2,1)} %refs_2_.2), custom_call_target="tpu_custom_call" | custom-call | flops 38654705664 | bytes 75497472 | tf_op jit(solution)/shard_map/k3/pallas_call | solution.py:84
  338.5 78.2 %k4.2 = (bf16[8192,1536]{1,0:T(8,128)(2,1)}, f32[768,1536]{1,0:T(8,128)}, f32[1536,768]{1,0:T(8,128)}) custom-call(bf16[8192,768]{1,0:T(8,128)(2,1)} %x_ref.5, bf16[8192,768]{1,0:T(8,128)(2,1)} %k3.2.dh2_ref.refs_3_, bf16[8192,3072]{1,0:T(8,128)(2,1)} %get-tuple-element.22.a1_ref, bf16[3072,768]{1,0:T(8,128)(2,1)} %w2_ref.5), custom_call_target="tpu_custom_call" | custom-call | flops 57982058496 | bytes 201326592 | tf_op jit(solution)/shard_map/k4/pallas_call | solution.py:113
  416.6 0.0 reduce-scatter.7.cloned.1.call-update
  416.7 0.0 reduce-scatter.15.cloned.1.call-start
  416.7 0.5 reduce-scatter.15.cloned.1.call-update
  417.2 0.0 reduce-scatter.13.cloned.1.call-start
  417.3 0.0 reduce-scatter.9.cloned.1.call-done
  417.3 13.8 %reduce-scatter.11.cloned.1.call-done = f32[384,768]{1,0:T(8,128)} async-done(((f32[3072,768]{1,0:T(8,128)}), f32[384,768]{1,0:T(8,128)}) %reduce-scatter.11.cloned.1.call-update) | async-done | bytes 1179664 | tf_op jit(solution)/shard_map/reduce_scatter | solution.py:128
  431.1 78.4 %k4.3 = (bf16[8192,1536]{1,0:T(8,128)(2,1)}, f32[768,1536]{1,0:T(8,128)}, f32[1536,768]{1,0:T(8,128)}) custom-call(bf16[8192,768]{1,0:T(8,128)(2,1)} %x_ref.5, bf16[8192,768]{1,0:T(8,128)(2,1)} %k3.2.dh2_ref.refs_3_, bf16[8192,3072]{1,0:T(8,128)(2,1)} %get-tuple-element.22.a1_ref, bf16[3072,768]{1,0:T(8,128)(2,1)} %w2_ref.5), custom_call_target="tpu_custom_call" | custom-call | flops 57982058496 | bytes 201326592 | tf_op jit(solution)/shard_map/k4/pallas_call | solution.py:113
  509.6 0.0 reduce-scatter.13.cloned.1.call-update
  509.6 0.0 reduce-scatter.17.cloned.1.call-start
  509.6 0.5 reduce-scatter.17.cloned.1.call-update
  510.2 0.0 all-gather.7.cloned.1.call-start
  510.2 0.0 reduce-scatter.7.cloned.1.call-done
  510.2 0.7 all-gather.7.cloned.1.call-update
  510.9 0.0 all-gather.11.cloned.1.call-start
  511.0 18.1 %reduce-scatter.15.cloned.1.call-done = f32[192,768]{1,0:T(8,128)} async-done(((f32[1536,768]{1,0:T(8,128)}), f32[192,768]{1,0:T(8,128)}) %reduce-scatter.15.cloned.1.call-update) | async-done | bytes 589840 | tf_op jit(solution)/shard_map/reduce_scatter | solution.py:128
  529.0 0.0 all-gather.11.cloned.1.call-update
  529.0 0.0 all-gather.9.cloned.1.call-start
  529.1 48.8 %reduce-scatter.13.cloned.1.call-done = f32[96,1536]{1,0:T(8,128)} async-done(((f32[768,1536]{1,0:T(8,128)}), f32[96,1536]{1,0:T(8,128)}) %reduce-scatter.13.cloned.1.call-update) | async-done | bytes 589840 | tf_op jit(solution)/shard_map/reduce_scatter | solution.py:128
  577.8 0.0 all-gather.9.cloned.1.call-update
  577.9 0.0 all-gather.13.cloned.1.call-start
  577.9 48.8 %reduce-scatter.17.cloned.1.call-done = f32[192,768]{1,0:T(8,128)} async-done(((f32[1536,768]{1,0:T(8,128)}), f32[192,768]{1,0:T(8,128)}) %reduce-scatter.17.cloned.1.call-update) | async-done | bytes 589840 | tf_op jit(solution)/shard_map/reduce_scatter | solution.py:128
  626.7 0.0 all-gather.13.cloned.1.call-update
  626.7 0.0 all-gather.15.cloned.1.call-start
  626.7 0.7 all-gather.15.cloned.1.call-update
  627.4 0.3 all-gather.17.cloned.1.call-start
  627.7 0.3 all-gather.17.cloned.1.call-update
  628.0 48.4 %k3.3 = bf16[8192,768]{1,0:T(8,128)(2,1)} custom-call(bf16[8192,1536]{1,0:T(8,128)(2,1)} %get-tuple-element.33.refs_0_, bf16[8192,1536]{1,0:T(8,128)(2,1)} %get-tuple-element.34.refs_1_, bf16[768,3072]{1,0:T(8,128)(2,1)} %refs_2_.3, bf16[8192,768]{1,0:T(8,128)(2,1)} %k3.2.dh2_ref.refs_3_), custom_call_target="tpu_custom_call" | custom-call | flops 38654705664 | bytes 75497472 | tf_op jit(solution)/shard_map/k3/pallas_call | solution.py:84
  676.4 0.0 all-gather.7.cloned.1.call-done
  676.4 5.0 broadcast_multiply_fusion.5
  681.4 14.9 %all-gather.11.cloned.1.call-done = f32[1536,768]{1,0:T(8,128)} async-done(((f32[192,768]{1,0:T(8,128)}), f32[1536,768]{1,0:T(8,128)}) %all-gather.11.cloned.1.call-update) | async-done | bytes 4718608 | tf_op jit(solution)/shard_map/all_gather | solution.py:131
  696.2 4.8 broadcast_multiply_fusion.3
  701.1 30.0 %all-gather.9.cloned.1.call-done = f32[768,1536]{1,0:T(8,128)} async-done(((f32[96,1536]{1,0:T(8,128)}), f32[768,1536]{1,0:T(8,128)}) %all-gather.9.cloned.1.call-update) | async-done | bytes 4718608 | tf_op jit(solution)/shard_map/all_gather | solution.py:131
  731.0 0.0 copy-start.1
  731.0 3.0 broadcast_multiply_fusion.4
  734.0 0.8 copy-done.1
  734.8 4.6 pad_maximum_fusion
  739.4 26.3 %all-gather.13.cloned.1.call-done = f32[1536,768]{1,0:T(8,128)} async-done(((f32[192,768]{1,0:T(8,128)}), f32[1536,768]{1,0:T(8,128)}) %all-gather.13.cloned.1.call-update) | async-done | bytes 4718608 | tf_op jit(solution)/shard_map/all_gather | solution.py:131
  765.7 0.0 copy-start
  765.7 2.8 broadcast_multiply_fusion.2
  768.5 0.9 copy-done
  769.4 4.3 pad_maximum_fusion.1
  773.8 46.7 %all-gather.15.cloned.1.call-done = f32[768,3072]{1,0:T(8,128)} async-done(((f32[96,3072]{1,0:T(8,128)}), f32[768,3072]{1,0:T(8,128)}) %all-gather.15.cloned.1.call-update) | async-done | bytes 9437200 | tf_op jit(solution)/shard_map/all_gather | solution.py:131
  820.5 9.1 %broadcast_multiply_fusion.1 = f32[768,3072]{1,0:T(8,128)} fusion(f32[768,3072]{1,0:T(8,128)} %all-gather.15.cloned.1.call-done), kind=kLoop, calls=%fused_computation.3 | loop fusion | flops 2359296 | bytes 18874368 | tf_op jit(solution)/shard_map/div | solution.py:131
  829.6 45.5 %all-gather.17.cloned.1.call-done = f32[3072,768]{1,0:T(8,128)} async-done(((f32[384,768]{1,0:T(8,128)}), f32[3072,768]{1,0:T(8,128)}) %all-gather.17.cloned.1.call-update) | async-done | bytes 9437200 | tf_op jit(solution)/shard_map/all_gather | solution.py:131
  875.1 8.0 broadcast_multiply_fusion
Async XLA Ops:
  7.2 410.1 %reduce-scatter.9.cloned.1.call-start = ((), (), s32[]{:S(2)}) async-start(), calls=%async_computation.8 | async-start | bytes 10616832 | tf_op jit(solution)/shard_map/reduce_scatter | solution.py:128
  289.2 141.9 %reduce-scatter.11.cloned.1.call-start = ((), (), s32[]{:S(2)}) async-start(), calls=%async_computation.9 | async-start | bytes 10616832 | tf_op jit(solution)/shard_map/reduce_scatter | solution.py:128
  290.0 220.2 %reduce-scatter.7.cloned.1.call-start = ((), (), s32[]{:S(2)}) async-start(), calls=%async_computation.6 | async-start | bytes 5308416 | tf_op jit(solution)/shard_map/reduce_scatter | solution.py:128
  416.7 112.4 %reduce-scatter.15.cloned.1.call-start = ((), (), s32[]{:S(2)}) async-start(), calls=%async_computation.12 | async-start | bytes 5308416 | tf_op jit(solution)/shard_map/reduce_scatter | solution.py:128
  417.2 160.6 %reduce-scatter.13.cloned.1.call-start = ((), (), s32[]{:S(2)}) async-start(), calls=%async_computation.10 | async-start | bytes 5308416 | tf_op jit(solution)/shard_map/reduce_scatter | solution.py:128
  509.6 117.1 %reduce-scatter.17.cloned.1.call-start = ((), (), s32[]{:S(2)}) async-start(), calls=%async_computation.14 | async-start | bytes 5308416 | tf_op jit(solution)/shard_map/reduce_scatter | solution.py:128
  510.2 166.2 %all-gather.7.cloned.1.call-start = ((), (), s32[]{:S(2)}) async-start(), calls=%async_computation.7 | async-start | bytes 5308416 | tf_op jit(solution)/shard_map/all_gather | solution.py:131
  510.9 185.3 %all-gather.11.cloned.1.call-start = ((), (), s32[]{:S(2)}) async-start(), calls=%async_computation.13 | async-start | bytes 5308416 | tf_op jit(solution)/shard_map/all_gather | solution.py:131
  529.0 202.0 %all-gather.9.cloned.1.call-start = ((), (), s32[]{:S(2)}) async-start(), calls=%async_computation.11 | async-start | bytes 5308416 | tf_op jit(solution)/shard_map/all_gather | solution.py:131
  577.9 187.8 %all-gather.13.cloned.1.call-start = ((), (), s32[]{:S(2)}) async-start(), calls=%async_computation.15 | async-start | bytes 5308416 | tf_op jit(solution)/shard_map/all_gather | solution.py:131
  626.7 193.8 %all-gather.15.cloned.1.call-start = ((), (), s32[]{:S(2)}) async-start(), calls=%async_computation.16 | async-start | bytes 10616832 | tf_op jit(solution)/shard_map/all_gather | solution.py:131
  627.4 247.7 %all-gather.17.cloned.1.call-start = ((), (), s32[]{:S(2)}) async-start(), calls=%async_computation.17 | async-start | bytes 10616832 | tf_op jit(solution)/shard_map/all_gather | solution.py:131
  731.0 3.8 copy-start.1
  765.7 3.8 copy-start
Sparse Core Ops, SparseCore 0:
  289.4 70.2 reduce-scatter.8
  363.7 67.4 reduce-scatter.10
  435.1 45.0 reduce-scatter.6
  484.0 45.0 reduce-scatter.14
  532.8 44.9 reduce-scatter.12
  581.6 44.9 reduce-scatter.16
  628.5 32.9 all-gather.6
  663.3 32.9 all-gather.10
  698.1 32.9 all-gather.8
  732.7 32.9 all-gather.12
  767.5 52.9 all-gather.14
  822.1 52.9 all-gather.16

commit v2 on v0

v2 whole, which is shorter than its diff:
```python
import functools

import jax
import jax.numpy as jnp
from jax import lax
from jax.experimental import pallas as pl
from jax.experimental.pallas import tpu as pltpu
from jax.sharding import PartitionSpec as P

f32 = jnp.float32
bf = jnp.bfloat16
D = 768
F = 3072
N = 8192
FC = 768
NC = F // FC
C1 = 0.7978845608028654
C2 = C1 * 0.044715
MESH = pl.DeviceIdType.MESH
HR, IR, JR = 384, 192, 96
VMEM_BYTES = 63 * 2**20


def nn(a, b):
    return lax.dot_general(a, b, (((1,), (0,)), ((), ())), preferred_element_type=f32)


def nt(a, b):
    return lax.dot_general(a, b, (((1,), (1,)), ((), ())), preferred_element_type=f32)


def tn(a, b):
    return lax.dot_general(a, b, (((0,), (0,)), ((), ())), preferred_element_type=f32)


def gelu_f(x):
    t = jnp.tanh(x * (C1 + C2 * (x * x)))
    return (0.5 * x) * (1.0 + t)


def gelu_both(x, d):
    x2 = x * x
    t = jnp.tanh(x * (C1 + C2 * x2))
    s = 1.0 + t
    hx = 0.5 * x
    w = ((1.0 - t) * s) * hx
    return hx * s, (0.5 * s + w * (C1 + (3.0 * C2) * x2)) * d


def k1(x_ref, w1_ref, w2_ref, a1_ref, h2_ref, h1_scr, *, sub, fch):
    for j in range(x_ref.shape[0] // sub):
        sl = pl.ds(j * sub, sub)
        for f in range(F // fch):
            fs = pl.ds(f * fch, fch)
            a1_ref[sl, fs] = nn(x_ref[sl, :], w1_ref[:, fs]).astype(bf)
            h1_scr[sl, fs] = gelu_f(a1_ref[sl, fs].astype(f32)).astype(bf)
        h2_ref[sl, :] = (nn(h1_scr[sl, :], w2_ref[...]) + x_ref[sl, :].astype(f32)).astype(bf)


def call_k1(x, w1, w2, R=512, sub=256, fch=768):
    return pl.pallas_call(
        functools.partial(k1, sub=sub, fch=fch),
        grid=(N // R,),
        in_specs=[pl.BlockSpec((R, D), lambda r: (r, 0)), pl.BlockSpec((D, F), lambda r: (0, 0)), pl.BlockSpec((F, D), lambda r: (0, 0))],
        out_specs=[pl.BlockSpec((R, F), lambda r: (r, 0)), pl.BlockSpec((R, D), lambda r: (r, 0))],
        out_shape=[jax.ShapeDtypeStruct((N, F), bf), jax.ShapeDtypeStruct((N, D), bf)],
        scratch_shapes=[pltpu.VMEM((R, F), bf)],
        compiler_params=pltpu.CompilerParams(vmem_limit_bytes=VMEM_BYTES),
        cost_estimate=pl.CostEstimate(flops=4 * N * D * F, bytes_accessed=2 * N * (F + 2 * D), transcendentals=N * F),
        name="k1",
    )(x, w1, w2)


def comm_scratch(slots):
    sem = pltpu.SemaphoreType.DMA
    return [
        pltpu.VMEM((slots, 2, FC, D), f32),
        pltpu.VMEM((2, FC, D), f32),
        pltpu.VMEM((2, 2, IR, D), f32),
        pltpu.VMEM((2, 2, JR, D), f32),
        pltpu.VMEM((2, FC, D), f32),
        sem((2, 2)),
        sem((4, 2, 2, 2)),
        sem((2, 3)),
        sem((2,)),
    ]


class Comm:
    def __init__(self, scr, red):
        self.acc, self.rx0, self.rx1, self.rx2, self.res, self.sem0, self.semx, self.sem5, self.seml = scr
        self.red = red
        self.a, self.b, self.c = lax.axis_index("dpa"), lax.axis_index("dpb"), lax.axis_index("dpc")
        self.mi, self.mj = (self.b, self.a), (self.a, self.b)
        x, y = {"dpb": 1 - self.b}, {"dpa": 1 - self.a}
        self.di, self.dj = (x, y), (y, x)
        self.dc = {"dpc": 1 - self.c}

    def barrier(self):
        sem = pltpu.get_barrier_semaphore()
        for dev in (self.di[0], self.di[1], self.dc):
            pl.semaphore_signal(sem, inc=1, device_id=dev, device_id_type=MESH)
        pl.semaphore_wait(sem, 3)

    def rows_i(self, h, i):
        return pl.ds(pl.multiple_of(h * HR + i * IR, JR), IR)

    def rows_j(self, h, i, j):
        return pl.ds(pl.multiple_of(h * HR + i * IR + j * JR, JR), JR)

    def p0(self, slot, aslot):
        return pltpu.make_async_remote_copy(self.acc.at[aslot, 1 - self.c], self.rx0.at[slot], self.sem0.at[slot, 0], self.sem0.at[slot, 1], device_id=self.dc, device_id_type=MESH)

    def px(self, phase, h, slot, aslot=None):
        i, j = self.mi[h], self.mj[h]
        if phase == 1:
            src, dst, dev = self.acc.at[aslot, self.c, self.rows_i(h, 1 - i)], self.rx1.at[slot, h], self.di[h]
        elif phase == 2:
            src, dst, dev = self.acc.at[aslot, self.c, self.rows_j(h, i, 1 - j)], self.rx2.at[slot, h], self.dj[h]
        elif phase == 3:
            src = dst = self.res.at[slot, self.rows_j(h, i, j)]
            dev = self.dj[h]
        else:
            src = dst = self.res.at[slot, self.rows_i(h, i)]
            dev = self.di[h]
        return pltpu.make_async_remote_copy(src, dst, self.semx.at[phase - 1, slot, h, 0], self.semx.at[phase - 1, slot, h, 1], device_id=dev, device_id_type=MESH)

    def p5(self, slot, idx):
        src, dst = self.res.at[slot], self.red.at[idx, self.c]
        return (
            pltpu.make_async_remote_copy(src, dst, self.sem5.at[slot, 0], self.sem5.at[slot, 1], device_id=self.dc, device_id_type=MESH),
            pltpu.make_async_copy(src, dst, self.sem5.at[slot, 2]),
        )

    def start0(self, slot, aslot):
        self.p0(slot, aslot).start()

    def start1(self, slot, aslot):
        self.p0(slot, aslot).wait()
        for h in range(2):
            sl = self.rows_i(h, 1 - self.mi[h])
            self.acc[aslot, self.c, sl, :] += self.rx0[slot, sl, :]
        for h in range(2):
            self.px(1, h, slot, aslot).start()
        for h in range(2):
            sl = self.rows_i(h, self.mi[h])
            self.acc[aslot, self.c, sl, :] += self.rx0[slot, sl, :]

    def start2(self, slot, aslot):
        for h in range(2):
            self.px(1, h, slot, aslot).wait()
        for h in range(2):
            sl = self.rows_i(h, self.mi[h])
            self.acc[aslot, self.c, sl, :] += self.rx1[slot, h]
        for h in range(2):
            self.px(2, h, slot, aslot).start()

    def start3(self, slot, aslot):
        for h in range(2):
            self.px(2, h, slot, aslot).wait()
        for h in range(2):
            sl = self.rows_j(h, self.mi[h], self.mj[h])
            self.res[slot, sl, :] = (self.acc[aslot, self.c, sl, :] + self.rx2[slot, h]) * 0.125
        for h in range(2):
            self.px(3, h, slot).start()

    def wait3(self, slot):
        for h in range(2):
            self.px(3, h, slot).wait()

    def start4(self, slot):
        for h in range(2):
            self.px(4, h, slot).start()

    def start5(self, slot, idx):
        for h in range(2):
            self.px(4, h, slot).wait()
        for cp in self.p5(slot, idx):
            cp.start()

    def wait5(self, slot, idx):
        for cp in self.p5(slot, idx):
            cp.wait()


def comm_steps(cm, c, s, ev, *, nseg, acc_in, res_in, slots):
    cur, fin = lax.rem(c + 1, 2), lax.rem(c, 2)
    aslot = cur if slots == 2 else 0
    nfin0 = 1 if res_in else 0
    idx = jnp.where(c == 0, 0, c - 2 + nfin0) if not acc_in else 0
    if acc_in:
        has_cur = has_fin = None
    else:
        has_cur = c >= 1
        has_fin = (c >= 2) | (c == 0) if res_in else c >= 2

    def at(step, cond, f):
        pred = s == step
        if cond is not None:
            pred = pred & cond
        pl.when(pred)(f)

    events = [
        (ev["s0"], has_cur, lambda: cm.start0(cur, aslot)),
        (ev["s4"], has_fin, lambda: cm.start4(fin)),
        (ev["s1"], has_cur, lambda: cm.start1(cur, aslot)),
        (ev["s5"], has_fin, lambda: cm.start5(fin, idx)),
        (ev["s2"], has_cur, lambda: cm.start2(cur, aslot)),
        (ev["w5"], has_fin, lambda: cm.wait5(fin, idx)),
        (ev["s3"], has_cur, lambda: cm.start3(cur, aslot)),
        (ev["w3"], has_cur, lambda: cm.wait3(cur)),
    ]
    for step, cond, f in sorted(events, key=lambda e: e[0]):
        at(step, cond, f)


def load(cm, acc_in, res_in):
    cps = []
    if acc_in is not None:
        cps.append(pltpu.make_async_copy(acc_in, cm.acc.at[0], cm.seml.at[0]))
    if res_in is not None:
        cps.append(pltpu.make_async_copy(res_in, cm.res.at[0], cm.seml.at[1]))
    for cp in cps:
        cp.start()
    for cp in cps:
        cp.wait()


def store(cm, acc_out, aslot, res_out, rslot):
    cps = []
    if acc_out is not None:
        cps.append(pltpu.make_async_copy(cm.acc.at[aslot], acc_out, cm.seml.at[0]))
    if res_out is not None:
        cps.append(pltpu.make_async_copy(cm.res.at[rslot], res_out, cm.seml.at[1]))
    for cp in cps:
        cp.start()
    for cp in cps:
        cp.wait()


EV = {"s0": 0, "s4": 0, "s1": 2, "s5": 6, "s2": 7, "w5": 8, "s3": 10, "w3": 13}


def accumulate(n, dd, ee, pp):
    for j in range(n):
        dd(j)
        if j > 0:
            ee(j - 1)
        if j > 1:
            pp(j - 2)
    ee(n - 1)
    if n > 1:
        pp(n - 2)
    pp(n - 1)


def k2(h2_ref, g_ref, w3_ref, w4_ref, da3_ref, red, acc_out, res_out, a_scr, d_scr, h_scr, *scr, sub, ev):
    c, s = pl.program_id(0), pl.program_id(1)
    cm = Comm(scr, red)
    acc = cm.acc
    pl.when((c == 0) & (s == 0))(cm.barrier)
    slot = lax.rem(c, 2)
    comm_steps(cm, c, s, ev, nseg=NC, acc_in=False, res_in=False, slots=2)

    @pl.when(s == 0)
    def _():
        acc[slot] = jnp.zeros(acc.shape[1:], f32)

    def dd(j):
        sl = pl.ds(j * sub, sub)
        a_scr[sl, :] = nn(h2_ref[sl, :], w3_ref[...]).astype(bf)
        d_scr[sl, :] = nt(g_ref[sl, :], w4_ref[...]).astype(bf)

    def ee(j):
        sl = pl.ds(j * sub, sub)
        h, da = gelu_both(a_scr[sl, :].astype(f32), d_scr[sl, :].astype(f32))
        h_scr[sl, :] = h.astype(bf)
        da3_ref[sl, :] = da.astype(bf)

    def pp(j):
        sl = pl.ds(j * sub, sub)
        acc[slot, 1] += tn(h_scr[sl, :], g_ref[sl, :])
        acc[slot, 0] += tn(h2_ref[sl, :], da3_ref[sl, :])

    accumulate(h2_ref.shape[0] // sub, dd, ee, pp)

    @pl.when((c == NC - 1) & (s == pl.num_programs(1) - 1))
    def _():
        store(cm, acc_out, (NC - 1) % 2, res_out, NC % 2)


def any_spec():
    return pl.BlockSpec(memory_space=pltpu.HBM)


def red_shape(n):
    return jax.ShapeDtypeStruct((n, 2, FC, D), f32)


ACC_SHAPE = jax.ShapeDtypeStruct((2, FC, D), f32)
RES_SHAPE = jax.ShapeDtypeStruct((FC, D), f32)


def params(cid):
    return pltpu.CompilerParams(vmem_limit_bytes=VMEM_BYTES, collective_id=cid, has_side_effects=True)


def call_k2(h2, g, w3, w4, R=512, sub=256):
    row = pl.BlockSpec((R, D), lambda c, r: (r, 0))
    return pl.pallas_call(
        functools.partial(k2, sub=sub, ev=EV),
        grid=(NC, N // R),
        in_specs=[row, row, pl.BlockSpec((D, FC), lambda c, r: (0, c)), pl.BlockSpec((FC, D), lambda c, r: (c, 0))],
        out_specs=[pl.BlockSpec((R, FC), lambda c, r: (r, c)), any_spec(), any_spec(), any_spec()],
        out_shape=[jax.ShapeDtypeStruct((N, F), bf), red_shape(2), ACC_SHAPE, RES_SHAPE],
        scratch_shapes=[pltpu.VMEM((R, FC), bf)] * 3 + comm_scratch(2),
        compiler_params=params(0),
        cost_estimate=pl.CostEstimate(flops=8 * N * D * F, bytes_accessed=2 * N * (F + 8 * D), transcendentals=N * F),
        name="k2",
    )(h2, g, w3, w4)


def k3(a_ref, w_ref, r_ref, acc_in, res_in, o_ref, red, *rest, sub, ev, last):
    res_out, scr = (None, rest) if last else (rest[0], rest[1:])
    s = pl.program_id(0)
    end = pl.num_programs(0) - 1
    cm = Comm(scr, red)

    @pl.when(s == 0)
    def _():
        load(cm, acc_in, res_in)
        cm.barrier()

    comm_steps(cm, 0, s, ev, nseg=1, acc_in=True, res_in=True, slots=1)
    for j in range(a_ref.shape[0] // sub):
        sl = pl.ds(j * sub, sub)
        o_ref[sl, :] = (nt(a_ref[sl, :], w_ref[...]) + r_ref[sl, :].astype(f32)).astype(bf)

    @pl.when(s == end)
    def _():
        if last:
            cm.start4(1)
            cm.start5(1, 1)
            cm.wait5(1, 1)
        else:
            store(cm, None, None, res_out, 1)


def call_k3(a, w, res, acc_in, res_in, last, cid, R=512, sub=256):
    row = pl.BlockSpec((R, D), lambda r: (r, 0))
    return pl.pallas_call(
        functools.partial(k3, sub=sub, ev=EV, last=last),
        grid=(N // R,),
        in_specs=[pl.BlockSpec((R, F), lambda r: (r, 0)), pl.BlockSpec((D, F), lambda r: (0, 0)), row, any_spec(), any_spec()],
        out_specs=[row, any_spec()] + ([] if last else [any_spec()]),
        out_shape=[jax.ShapeDtypeStruct((N, D), bf), red_shape(2 if last else 1)] + ([] if last else [RES_SHAPE]),
        scratch_shapes=comm_scratch(1),
        compiler_params=params(cid),
        cost_estimate=pl.CostEstimate(flops=2 * N * D * F, bytes_accessed=2 * N * (F + 2 * D), transcendentals=0),
        name="k5" if last else "k3",
    )(a, w, res, acc_in, res_in)


def k4(x_ref, dh2_ref, a1_ref, w2_ref, res_in, da1_ref, red, acc_out, res_out, d_scr, h_scr, *scr, sub, ev):
    c, s = pl.program_id(0), pl.program_id(1)
    cm = Comm(scr, red)
    acc = cm.acc

    @pl.when((c == 0) & (s == 0))
    def _():
        load(cm, None, res_in)
        cm.barrier()

    slot = lax.rem(c, 2)
    comm_steps(cm, c, s, ev, nseg=NC, acc_in=False, res_in=True, slots=2)

    @pl.when(s == 0)
    def _():
        acc[slot] = jnp.zeros(acc.shape[1:], f32)

    def dd(j):
        sl = pl.ds(j * sub, sub)
        d_scr[sl, :] = nt(dh2_ref[sl, :], w2_ref[...]).astype(bf)

    def ee(j):
        sl = pl.ds(j * sub, sub)
        h, da = gelu_both(a1_ref[sl, :].astype(f32), d_scr[sl, :].astype(f32))
        h_scr[sl, :] = h.astype(bf)
        da1_ref[sl, :] = da.astype(bf)

    def pp(j):
        sl = pl.ds(j * sub, sub)
        acc[slot, 1] += tn(h_scr[sl, :], dh2_ref[sl, :])
        acc[slot, 0] += tn(x_ref[sl, :], da1_ref[sl, :])

    accumulate(x_ref.shape[0] // sub, dd, ee, pp)

    @pl.when((c == NC - 1) & (s == pl.num_programs(1) - 1))
    def _():
        store(cm, acc_out, (NC - 1) % 2, res_out, NC % 2)


def call_k4(x, dh2, a1, w2, res_in, R=512, sub=256):
    row = pl.BlockSpec((R, D), lambda c, r: (r, 0))
    blk = pl.BlockSpec((R, FC), lambda c, r: (r, c))
    return pl.pallas_call(
        functools.partial(k4, sub=sub, ev=EV),
        grid=(NC, N // R),
        in_specs=[row, row, blk, pl.BlockSpec((FC, D), lambda c, r: (c, 0)), any_spec()],
        out_specs=[blk, any_spec(), any_spec(), any_spec()],
        out_shape=[jax.ShapeDtypeStruct((N, F), bf), red_shape(3), ACC_SHAPE, RES_SHAPE],
        scratch_shapes=[pltpu.VMEM((R, FC), bf)] * 2 + comm_scratch(2),
        compiler_params=params(2),
        cost_estimate=pl.CostEstimate(flops=6 * N * D * F, bytes_accessed=2 * N * (2 * F + 8 * D), transcendentals=N * F),
        name="k4",
    )(x, dh2, a1, w2, res_in)


def place(r2, r3, r4a, r4b, r5, dx_in, dw1, dw2, dw3, dw4, dx):
    c = pl.program_id(0) // 4
    dx[...] = dx_in[...]

    def put(cond, src, wa, wb):
        @pl.when(cond)
        def _():
            wa[...] = src[0, 0]
            wb[...] = src[0, 1]

    put(c < 2, r2, dw3, dw4)
    put(c == 2, r3, dw3, dw4)
    put(c == 3, r4a, dw3, dw4)
    put(c < 2, r4b, dw1, dw2)
    put(c >= 2, r5, dw1, dw2)


def call_place(r2, r3, r4, r5, dx):
    rows = FC // 4

    def spec(lo, n, first):
        def index(t):
            k = jnp.clip(t, 4 * lo, 4 * (lo + n) - 1)
            return first + k // 4 - lo, 0, lax.rem(k, 4), 0

        return pl.BlockSpec((1, 2, rows, D), index)

    row = pl.BlockSpec((N // 16, D), lambda t: (t, 0))
    wide = pl.BlockSpec((rows, FC), lambda t: (lax.rem(t, 4), t // 4))
    tall = pl.BlockSpec((rows, D), lambda t: (t, 0))
    return pl.pallas_call(
        place,
        grid=(16,),
        in_specs=[spec(0, 2, 0), spec(2, 1, 0), spec(3, 1, 0), spec(0, 2, 1), spec(2, 2, 0), row],
        out_specs=[wide, tall, wide, tall, row],
        out_shape=[jax.ShapeDtypeStruct((D, F), f32), jax.ShapeDtypeStruct((F, D), f32)] * 2 + [jax.ShapeDtypeStruct((N, D), bf)],
        compiler_params=pltpu.CompilerParams(vmem_limit_bytes=VMEM_BYTES),
        name="place",
    )(r2, r3, r4, r4, r5, dx)


def solution(mesh):
    rows = P(("mp", "dpa", "dpb", "dpc"), None)
    wspec = P("mp", None)

    def local(x, g, w1, w2, w3, w4):
        a1, h2 = call_k1(x, w1, w2)
        da3, r2, acc, res = call_k2(h2, g, w3, w4)
        dh2, r3, res = call_k3(da3, w3, g, acc, res, False, 1)
        da1, r4, acc, res = call_k4(x, dh2, a1, w2, res)
        dx, r5 = call_k3(da1, w1, dh2, acc, res, True, 3)
        return tuple(call_place(r2, r3, r4, r5, dx))

    return jax.shard_map(local, mesh=mesh, in_specs=(rows, rows, wspec, wspec, wspec, wspec), out_specs=(wspec, wspec, wspec, wspec, rows), check_vma=False)
```

time: 1110 us -> 695 us (0.63)
  Pallas kernels: 0 us -> 694 us
  matrix products: 680 us -> 0 us
  waiting for transfers between devices: 354 us -> 0 us
  other arithmetic: 32.1 us -> 0 us
  local copies, waits for them, and re-layouts: 19.2 us -> 0 us
  between operations: 14.1 us -> 0.66 us
    pallas_call x0 -> x6, Pallas kernels: none -> 694 us  [the longest x1 220 us: call_k2(): pl.pallas_call(functools.partial(k2, sub=sub, ev=EV), grid=(NC, N // R),...]
    dot_general x11 -> x0, matrix products: 680 us -> none  [the longest x1 98.8 us: local(): dh3 = jnp.dot(g, w4.T, preferred_element_type=f32).astype(bf)]
    psum x1 -> x0, waiting for transfers between devices: 335 us -> none  [reduce_grad(): s = lax.psum(s, ('dpa', 'dpb'))]
    div x4 -> x0, other arithmetic: 32.1 us -> none  [reduce_grad(): return lax.all_gather(s, 'dpc', axis=0, tiled=True) / ndev]
    unnamed x8 -> x0, local copies, waits for them, and re-layouts: 19.2 us -> none
    reduce_scatter x4 -> x0, waiting for transfers between devices: 16.8 us -> none  [reduce_grad(): s = lax.psum_scatter(dw, 'dpc', scatter_dimension=0, tiled=True)]
  transfers between devices with their start and end apart: 9 -> 0, of which waited for: 2 -> 0; matrix products, arithmetic and copies ran while one was open for 37% -> 0% of each run, Pallas kernels for 0% -> 0%
where the time goes in v2:
time: 695 us
  Pallas kernels  694 us (100%)
    pallas_call x1, Pallas kernels, call_k2(): pl.pallas_call(functools.partial(k2, sub=sub, ev=EV), grid=(NC, N // R),...  220 us
    pallas_call x1, Pallas kernels, call_k4(): pl.pallas_call(functools.partial(k4, sub=sub, ev=EV), grid=(NC, N // R),...  207 us
    pallas_call x2, Pallas kernels, call_k3(): pl.pallas_call(functools.partial(k3, sub=sub, ev=EV, last=last), grid=(N...  140 us
    pallas_call x1, Pallas kernels, call_k1(): pl.pallas_call(functools.partial(k1, sub=sub, fch=fch), grid=(N // R,), i...  89.6 us
    pallas_call x1, Pallas kernels, call_place(): pl.pallas_call(place, grid=(16,), in_specs=[spec(0, 2, 0), spec(2, 1, 0),...  37 us

profile of v2, /device:TPU:0, one launch (start us, length us, event | category | flops | bytes accessed | tf_op | source)
XLA Modules:
  0.0 694.8 jit_solution(6439062648935613786)
XLA Ops:
  0.6 89.6 %k1.1 = (bf16[8192,3072]{1,0:T(8,128)(2,1)}, bf16[8192,768]{1,0:T(8,128)(2,1)}) custom-call(bf16[8192,768]{1,0:T(8,128)(2,1)} %x_ref.3, bf16[768,3072]{1,0:T(8,128)(2,1)} %w_ref.3, bf16[3072,768]{1,0:T(8,128)(2,1)} %w2_ref.3), custom_call_target="tpu_custom_call" | custom-call | flops 77309411328 | bytes 75497472 | tf_op jit(solution)/shard_map/k1/pallas_call | solution.py:61
  90.3 220.3 %k2.1 = (bf16[8192,3072]{1,0:T(8,128)(2,1)}, f32[2,2,768,768]{3,2,1,0:T(8,128)}, f32[2,768,768]{2,1,0:T(8,128)}, f32[768,768]{1,0:T(8,128)}) custom-call(bf16[8192,768]{1,0:T(8,128)(2,1)} %get-tuple-element.20.h2_ref, bf16[8192,768]{1,0:T(8,128)(2,1)} %r_ref.1, bf16[768,3072]{1,0:T(8,128)(2,1)} %w_ref.2, bf16[3072,768]{1,0:T(8,128)(2,1)} %w4_ref.1), custom_call_target="tpu_custom_call" | custom-call | flops 154618822656 | bytes 150994944 | tf_op jit(solution)/shard_map/k2/pallas_call | solution.py:310
  310.6 60.2 %k3.1 = (bf16[8192,768]{1,0:T(8,128)(2,1)}, f32[1,2,768,768]{3,2,1,0:T(8,128)}, f32[768,768]{1,0:T(8,128)}) custom-call(bf16[8192,3072]{1,0:T(8,128)(2,1)} %get-tuple-element.22.a_ref, bf16[768,3072]{1,0:T(8,128)(2,1)} %w_ref.2, bf16[8192,768]{1,0:T(8,128)(2,1)} %r_ref.1, f32[2,768,768]{2,1,0:T(8,128)} %get-tuple-element.23.acc_in, ...), custom_call_target="tpu_custom_call" | custom-call | flops 38654705664 | bytes 75497472 | tf_op jit(solution)/shard_map/k3/pallas_call | solution.py:351
  370.8 207.0 %k4.1 = (bf16[8192,3072]{1,0:T(8,128)(2,1)}, f32[3,2,768,768]{3,2,1,0:T(8,128)}, f32[2,768,768]{2,1,0:T(8,128)}, f32[768,768]{1,0:T(8,128)}) custom-call(bf16[8192,768]{1,0:T(8,128)(2,1)} %x_ref.3, bf16[8192,768]{1,0:T(8,128)(2,1)} %get-tuple-element.26.dh2_ref.r_ref, bf16[8192,3072]{1,0:T(8,128)(2,1)} %get-tuple-element.27.a1_ref, ...), custom_call_target="tpu_custom_call" | custom-call | flops 115964116992 | bytes 201326592 | tf_op jit(solution)/shard_map/k4/pallas_call | solution.py:406
  577.8 80.0 %k5.1 = (bf16[8192,768]{1,0:T(8,128)(2,1)}, f32[2,2,768,768]{3,2,1,0:T(8,128)}) custom-call(bf16[8192,3072]{1,0:T(8,128)(2,1)} %get-tuple-element.30.a_ref, bf16[768,3072]{1,0:T(8,128)(2,1)} %w_ref.3, bf16[8192,768]{1,0:T(8,128)(2,1)} %get-tuple-element.26.dh2_ref.r_ref, f32[2,768,768]{2,1,0:T(8,128)} %get-tuple-element.31.acc_in, ...), custom_call_target="tpu_custom_call" | custom-call | flops 38654705664 | bytes 75497472 | tf_op jit(solution)/shard_map/k5/pallas_call | solution.py:351
  657.8 37.0 %place.1 = (f32[768,3072]{1,0:T(8,128)}, f32[3072,768]{1,0:T(8,128)}, f32[768,3072]{1,0:T(8,128)}, f32[3072,768]{1,0:T(8,128)}, bf16[8192,768]{1,0:T(8,128)(2,1)}) custom-call(f32[2,2,768,768]{3,2,1,0:T(8,128)} %get-tuple-element.21.r2, f32[1,2,768,768]{3,2,1,0:T(8,128)} %get-tuple-element.25.r3, f32[3,2,768,768]{3,2,1,0:T(8,128)} %get-tuple-element.29.r4a.r4b, ...), custom_call_target="tpu_custom_call" | custom-call | tf_op jit(solution)/shard_map/place/pallas_call | solution.py:449

commit v3 on v2

--- a/solution.py
+++ b/solution.py
@@ -57,7 +57,7 @@
         h2_ref[sl, :] = (nn(h1_scr[sl, :], w2_ref[...]) + x_ref[sl, :].astype(f32)).astype(bf)
 
 
-def call_k1(x, w1, w2, R=512, sub=256, fch=768):
+def call_k1(x, w1, w2, R=1024, sub=256, fch=768):
     return pl.pallas_call(
         functools.partial(k1, sub=sub, fch=fch),
         grid=(N // R,),
@@ -155,20 +155,20 @@
         for h in range(2):
             self.px(2, h, slot, aslot).start()
 
-    def start3(self, slot, aslot):
+    def end2(self, slot, aslot):
         for h in range(2):
             self.px(2, h, slot, aslot).wait()
         for h in range(2):
             sl = self.rows_j(h, self.mi[h], self.mj[h])
             self.res[slot, sl, :] = (self.acc[aslot, self.c, sl, :] + self.rx2[slot, h]) * 0.125
+
+    def start3(self, slot):
         for h in range(2):
             self.px(3, h, slot).start()
 
-    def wait3(self, slot):
+    def start4(self, slot):
         for h in range(2):
             self.px(3, h, slot).wait()
-
-    def start4(self, slot):
         for h in range(2):
             self.px(4, h, slot).start()
 
@@ -183,35 +183,31 @@
             cp.wait()
 
 
-def comm_steps(cm, c, s, ev, *, nseg, acc_in, res_in, slots):
+def comm_steps(cm, c, t, ev, *, acc_in, res_in, slots, end=False):
     cur, fin = lax.rem(c + 1, 2), lax.rem(c, 2)
     aslot = cur if slots == 2 else 0
-    nfin0 = 1 if res_in else 0
-    idx = jnp.where(c == 0, 0, c - 2 + nfin0) if not acc_in else 0
     if acc_in:
         has_cur = has_fin = None
+        idx = 0
     else:
         has_cur = c >= 1
         has_fin = (c >= 2) | (c == 0) if res_in else c >= 2
-
-    def at(step, cond, f):
-        pred = s == step
-        if cond is not None:
-            pred = pred & cond
-        pl.when(pred)(f)
-
+        idx = jnp.where(c == 0, 0, c - 1) if res_in else jnp.maximum(c - 2, 0)
     events = [
-        (ev["s0"], has_cur, lambda: cm.start0(cur, aslot)),
-        (ev["s4"], has_fin, lambda: cm.start4(fin)),
-        (ev["s1"], has_cur, lambda: cm.start1(cur, aslot)),
-        (ev["s5"], has_fin, lambda: cm.start5(fin, idx)),
-        (ev["s2"], has_cur, lambda: cm.start2(cur, aslot)),
-        (ev["w5"], has_fin, lambda: cm.wait5(fin, idx)),
-        (ev["s3"], has_cur, lambda: cm.start3(cur, aslot)),
-        (ev["w3"], has_cur, lambda: cm.wait3(cur)),
+        ("s0", has_cur, lambda: cm.start0(cur, aslot)),
+        ("s3", has_fin, lambda: cm.start3(fin)),
+        ("s1", has_cur, lambda: cm.start1(cur, aslot)),
+        ("s4", has_fin, lambda: cm.start4(fin)),
+        ("s2", has_cur, lambda: cm.start2(cur, aslot)),
+        ("s5", has_fin, lambda: cm.start5(fin, idx)),
+        ("w5", has_fin, lambda: cm.wait5(fin, idx)),
+        ("e2", has_cur, lambda: cm.end2(cur, aslot)),
     ]
-    for step, cond, f in sorted(events, key=lambda e: e[0]):
-        at(step, cond, f)
+    for key, cond, f in sorted(events, key=lambda e: ev[e[0]]):
+        if (ev[key] >= SLOTS) != end:
+            continue
+        pred = t == (SLOTS - 1 if end else ev[key])
+        pl.when(pred if cond is None else pred & cond)(f)
 
 
 def load(cm, acc_in, res_in):
@@ -238,7 +234,24 @@
         cp.wait()
 
 
-EV = {"s0": 0, "s4": 0, "s1": 2, "s5": 6, "s2": 7, "w5": 8, "s3": 10, "w3": 13}
+SLOTS = 8
+SR = N // SLOTS
+EV = {"s0": 0, "s3": 0, "s1": 1, "s4": 2, "s2": 5, "s5": 6, "w5": 7, "e2": 8}
+EV4 = {"s0": 0, "s3": 0, "s1": 1, "s4": 2, "s2": 6, "s5": 7, "w5": 8, "e2": 8}
+EV5 = {"s0": 0, "s3": 0, "s1": 1, "s4": 2, "s2": 5, "s5": 6, "w5": 7, "e2": 7}
+
+
+def slots_of(rows, body):
+    n = rows // SR
+
+    def one(i, carry):
+        body(i, pl.multiple_of(i * SR, SR))
+        return carry
+
+    if n == 1:
+        body(0, 0)
+    else:
+        lax.fori_loop(0, n, one, 0)
 
 
 def accumulate(n, dd, ee, pp):
@@ -260,29 +273,36 @@
     acc = cm.acc
     pl.when((c == 0) & (s == 0))(cm.barrier)
     slot = lax.rem(c, 2)
-    comm_steps(cm, c, s, ev, nseg=NC, acc_in=False, res_in=False, slots=2)
-
-    @pl.when(s == 0)
-    def _():
-        acc[slot] = jnp.zeros(acc.shape[1:], f32)
-
-    def dd(j):
-        sl = pl.ds(j * sub, sub)
-        a_scr[sl, :] = nn(h2_ref[sl, :], w3_ref[...]).astype(bf)
-        d_scr[sl, :] = nt(g_ref[sl, :], w4_ref[...]).astype(bf)
-
-    def ee(j):
-        sl = pl.ds(j * sub, sub)
-        h, da = gelu_both(a_scr[sl, :].astype(f32), d_scr[sl, :].astype(f32))
-        h_scr[sl, :] = h.astype(bf)
-        da3_ref[sl, :] = da.astype(bf)
-
-    def pp(j):
-        sl = pl.ds(j * sub, sub)
-        acc[slot, 1] += tn(h_scr[sl, :], g_ref[sl, :])
-        acc[slot, 0] += tn(h2_ref[sl, :], da3_ref[sl, :])
-
-    accumulate(h2_ref.shape[0] // sub, dd, ee, pp)
+    n = h2_ref.shape[0] // SR
+
+    def body(i, r0):
+        t = s * n + i
+        comm_steps(cm, c, t, ev, acc_in=False, res_in=False, slots=2)
+
+        @pl.when(t == 0)
+        def _():
+            acc[slot] = jnp.zeros(acc.shape[1:], f32)
+
+        def dd(j):
+            sl, ss = pl.ds(r0 + j * sub, sub), pl.ds(j * sub, sub)
+            a_scr[ss, :] = nn(h2_ref[sl, :], w3_ref[...]).astype(bf)
+            d_scr[ss, :] = nt(g_ref[sl, :], w4_ref[...]).astype(bf)
+
+        def ee(j):
+            sl, ss = pl.ds(r0 + j * sub, sub), pl.ds(j * sub, sub)
+            h, da = gelu_both(a_scr[ss, :].astype(f32), d_scr[ss, :].astype(f32))
+            h_scr[ss, :] = h.astype(bf)
+            da3_ref[sl, :] = da.astype(bf)
+
+        def pp(j):
+            sl, ss = pl.ds(r0 + j * sub, sub), pl.ds(j * sub, sub)
+            acc[slot, 1] += tn(h_scr[ss, :], g_ref[sl, :])
+            acc[slot, 0] += tn(h2_ref[sl, :], da3_ref[sl, :])
+
+        accumulate(SR // sub, dd, ee, pp)
+        comm_steps(cm, c, t, ev, acc_in=False, res_in=False, slots=2, end=True)
+
+    slots_of(h2_ref.shape[0], body)
 
     @pl.when((c == NC - 1) & (s == pl.num_programs(1) - 1))
     def _():
@@ -305,7 +325,7 @@
     return pltpu.CompilerParams(vmem_limit_bytes=VMEM_BYTES, collective_id=cid, has_side_effects=True)
 
 
-def call_k2(h2, g, w3, w4, R=512, sub=256):
+def call_k2(h2, g, w3, w4, R=1024, sub=256):
     row = pl.BlockSpec((R, D), lambda c, r: (r, 0))
     return pl.pallas_call(
         functools.partial(k2, sub=sub, ev=EV),
@@ -313,7 +333,7 @@
         in_specs=[row, row, pl.BlockSpec((D, FC), lambda c, r: (0, c)), pl.BlockSpec((FC, D), lambda c, r: (c, 0))],
         out_specs=[pl.BlockSpec((R, FC), lambda c, r: (r, c)), any_spec(), any_spec(), any_spec()],
         out_shape=[jax.ShapeDtypeStruct((N, F), bf), red_shape(2), ACC_SHAPE, RES_SHAPE],
-        scratch_shapes=[pltpu.VMEM((R, FC), bf)] * 3 + comm_scratch(2),
+        scratch_shapes=[pltpu.VMEM((SR, FC), bf)] * 3 + comm_scratch(2),
         compiler_params=params(0),
         cost_estimate=pl.CostEstimate(flops=8 * N * D * F, bytes_accessed=2 * N * (F + 8 * D), transcendentals=N * F),
         name="k2",
@@ -323,7 +343,6 @@
 def k3(a_ref, w_ref, r_ref, acc_in, res_in, o_ref, red, *rest, sub, ev, last):
     res_out, scr = (None, rest) if last else (rest[0], rest[1:])
     s = pl.program_id(0)
-    end = pl.num_programs(0) - 1
     cm = Comm(scr, red)
 
     @pl.when(s == 0)
@@ -331,12 +350,21 @@
         load(cm, acc_in, res_in)
         cm.barrier()
 
-    comm_steps(cm, 0, s, ev, nseg=1, acc_in=True, res_in=True, slots=1)
-    for j in range(a_ref.shape[0] // sub):
-        sl = pl.ds(j * sub, sub)
-        o_ref[sl, :] = (nt(a_ref[sl, :], w_ref[...]) + r_ref[sl, :].astype(f32)).astype(bf)
-
-    @pl.when(s == end)
+    n = a_ref.shape[0] // SR
+
+    def body(i, r0):
+        t = s * n + i
+        comm_steps(cm, 0, t, ev, acc_in=True, res_in=True, slots=1)
+        if last:
+            pl.when(t == ev["e2"])(lambda: cm.start3(1))
+        for j in range(SR // sub):
+            sl = pl.ds(r0 + j * sub, sub)
+            o_ref[sl, :] = (nt(a_ref[sl, :], w_ref[...]) + r_ref[sl, :].astype(f32)).astype(bf)
+        comm_steps(cm, 0, t, ev, acc_in=True, res_in=True, slots=1, end=True)
+
+    slots_of(a_ref.shape[0], body)
+
+    @pl.when(s == pl.num_programs(0) - 1)
     def _():
         if last:
             cm.start4(1)
@@ -346,10 +374,10 @@
             store(cm, None, None, res_out, 1)
 
 
-def call_k3(a, w, res, acc_in, res_in, last, cid, R=512, sub=256):
+def call_k3(a, w, res, acc_in, res_in, last, cid, R=1024, sub=512):
     row = pl.BlockSpec((R, D), lambda r: (r, 0))
     return pl.pallas_call(
-        functools.partial(k3, sub=sub, ev=EV, last=last),
+        functools.partial(k3, sub=sub, ev=EV5 if last else EV, last=last),
         grid=(N // R,),
         in_specs=[pl.BlockSpec((R, F), lambda r: (r, 0)), pl.BlockSpec((D, F), lambda r: (0, 0)), row, any_spec(), any_spec()],
         out_specs=[row, any_spec()] + ([] if last else [any_spec()]),
@@ -372,44 +400,51 @@
         cm.barrier()
 
     slot = lax.rem(c, 2)
-    comm_steps(cm, c, s, ev, nseg=NC, acc_in=False, res_in=True, slots=2)
-
-    @pl.when(s == 0)
-    def _():
-        acc[slot] = jnp.zeros(acc.shape[1:], f32)
-
-    def dd(j):
-        sl = pl.ds(j * sub, sub)
-        d_scr[sl, :] = nt(dh2_ref[sl, :], w2_ref[...]).astype(bf)
-
-    def ee(j):
-        sl = pl.ds(j * sub, sub)
-        h, da = gelu_both(a1_ref[sl, :].astype(f32), d_scr[sl, :].astype(f32))
-        h_scr[sl, :] = h.astype(bf)
-        da1_ref[sl, :] = da.astype(bf)
-
-    def pp(j):
-        sl = pl.ds(j * sub, sub)
-        acc[slot, 1] += tn(h_scr[sl, :], dh2_ref[sl, :])
-        acc[slot, 0] += tn(x_ref[sl, :], da1_ref[sl, :])
-
-    accumulate(x_ref.shape[0] // sub, dd, ee, pp)
+    n = x_ref.shape[0] // SR
+
+    def body(i, r0):
+        t = s * n + i
+        comm_steps(cm, c, t, ev, acc_in=False, res_in=True, slots=2)
+
+        @pl.when(t == 0)
+        def _():
+            acc[slot] = jnp.zeros(acc.shape[1:], f32)
+
+        def dd(j):
+            sl, ss = pl.ds(r0 + j * sub, sub), pl.ds(j * sub, sub)
+            d_scr[ss, :] = nt(dh2_ref[sl, :], w2_ref[...]).astype(bf)
+
+        def ee(j):
+            sl, ss = pl.ds(r0 + j * sub, sub), pl.ds(j * sub, sub)
+            h, da = gelu_both(a1_ref[sl, :].astype(f32), d_scr[ss, :].astype(f32))
+            h_scr[ss, :] = h.astype(bf)
+            da1_ref[sl, :] = da.astype(bf)
+
+        def pp(j):
+            sl, ss = pl.ds(r0 + j * sub, sub), pl.ds(j * sub, sub)
+            acc[slot, 1] += tn(h_scr[ss, :], dh2_ref[sl, :])
+            acc[slot, 0] += tn(x_ref[sl, :], da1_ref[sl, :])
+
+        accumulate(SR // sub, dd, ee, pp)
+        comm_steps(cm, c, t, ev, acc_in=False, res_in=True, slots=2, end=True)
+
+    slots_of(x_ref.shape[0], body)
 
     @pl.when((c == NC - 1) & (s == pl.num_programs(1) - 1))
     def _():
         store(cm, acc_out, (NC - 1) % 2, res_out, NC % 2)
 
 
-def call_k4(x, dh2, a1, w2, res_in, R=512, sub=256):
+def call_k4(x, dh2, a1, w2, res_in, R=1024, sub=512):
     row = pl.BlockSpec((R, D), lambda c, r: (r, 0))
     blk = pl.BlockSpec((R, FC), lambda c, r: (r, c))
     return pl.pallas_call(
-        functools.partial(k4, sub=sub, ev=EV),
+        functools.partial(k4, sub=sub, ev=EV4),
         grid=(NC, N // R),
         in_specs=[row, row, blk, pl.BlockSpec((FC, D), lambda c, r: (c, 0)), any_spec()],
         out_specs=[blk, any_spec(), any_spec(), any_spec()],
         out_shape=[jax.ShapeDtypeStruct((N, F), bf), red_shape(3), ACC_SHAPE, RES_SHAPE],
-        scratch_shapes=[pltpu.VMEM((R, FC), bf)] * 2 + comm_scratch(2),
+        scratch_shapes=[pltpu.VMEM((SR, FC), bf)] * 2 + comm_scratch(2),
         compiler_params=params(2),
         cost_estimate=pl.CostEstimate(flops=6 * N * D * F, bytes_accessed=2 * N * (2 * F + 8 * D), transcendentals=N * F),
         name="k4",

time: 695 us -> 628 us (0.904)
  Pallas kernels: 694 us -> 627 us
    pallas_call x3, Pallas kernels: 347 us -> 298 us  [the longest x1 165 us: call_k4(): pl.pallas_call(functools.partial(k4, sub=sub, ev=EV4), grid=(NC, N // R),...]
    pallas_call x1, Pallas kernels: 220 us -> 202 us  [call_k2(): pl.pallas_call(functools.partial(k2, sub=sub, ev=EV), grid=(NC, N // R),...]
where the time goes in v3:
time: 628 us
  Pallas kernels  627 us (100%)
    pallas_call x1, Pallas kernels, call_k2(): pl.pallas_call(functools.partial(k2, sub=sub, ev=EV), grid=(NC, N // R),...  202 us
    pallas_call x1, Pallas kernels, call_k4(): pl.pallas_call(functools.partial(k4, sub=sub, ev=EV4), grid=(NC, N // R),...  165 us
    pallas_call x2, Pallas kernels, call_k3(): pl.pallas_call(functools.partial(k3, sub=sub, ev=EV5 if last else EV, las...  133 us
    pallas_call x1, Pallas kernels, call_k1(): pl.pallas_call(functools.partial(k1, sub=sub, fch=fch), grid=(N // R,), i...  89 us
    pallas_call x1, Pallas kernels, call_place(): pl.pallas_call(place, grid=(16,), in_specs=[spec(0, 2, 0), spec(2, 1, 0),...  37 us

profile of v3, /device:TPU:0, one launch (start us, length us, event | category | flops | bytes accessed | tf_op | source)
XLA Modules:
  0.0 627.5 jit_solution(17627934957261535264)
XLA Ops:
  0.6 89.0 %k1.1 = (bf16[8192,3072]{1,0:T(8,128)(2,1)}, bf16[8192,768]{1,0:T(8,128)(2,1)}) custom-call(bf16[8192,768]{1,0:T(8,128)(2,1)} %x_ref.3, bf16[768,3072]{1,0:T(8,128)(2,1)} %w_ref.3, bf16[3072,768]{1,0:T(8,128)(2,1)} %w2_ref.3), custom_call_target="tpu_custom_call" | custom-call | flops 77309411328 | bytes 75497472 | tf_op jit(solution)/shard_map/k1/pallas_call | solution.py:61
  89.6 202.4 %k2.1 = (bf16[8192,3072]{1,0:T(8,128)(2,1)}, f32[2,2,768,768]{3,2,1,0:T(8,128)}, f32[2,768,768]{2,1,0:T(8,128)}, f32[768,768]{1,0:T(8,128)}) custom-call(bf16[8192,768]{1,0:T(8,128)(2,1)} %get-tuple-element.20.h2_ref, bf16[8192,768]{1,0:T(8,128)(2,1)} %r_ref.1, bf16[768,3072]{1,0:T(8,128)(2,1)} %w_ref.2, bf16[3072,768]{1,0:T(8,128)(2,1)} %w4_ref.1), custom_call_target="tpu_custom_call" | custom-call | flops 154618822656 | bytes 150994944 | tf_op jit(solution)/shard_map/k2/pallas_call | solution.py:330
  292.1 57.6 %k3.1 = (bf16[8192,768]{1,0:T(8,128)(2,1)}, f32[1,2,768,768]{3,2,1,0:T(8,128)}, f32[768,768]{1,0:T(8,128)}) custom-call(bf16[8192,3072]{1,0:T(8,128)(2,1)} %get-tuple-element.22.a_ref, bf16[768,3072]{1,0:T(8,128)(2,1)} %w_ref.2, bf16[8192,768]{1,0:T(8,128)(2,1)} %r_ref.1, f32[2,768,768]{2,1,0:T(8,128)} %get-tuple-element.23.acc_in, ...), custom_call_target="tpu_custom_call" | custom-call | flops 38654705664 | bytes 75497472 | tf_op jit(solution)/shard_map/k3/pallas_call | solution.py:379
  349.7 165.0 %k4.1 = (bf16[8192,3072]{1,0:T(8,128)(2,1)}, f32[3,2,768,768]{3,2,1,0:T(8,128)}, f32[2,768,768]{2,1,0:T(8,128)}, f32[768,768]{1,0:T(8,128)}) custom-call(bf16[8192,768]{1,0:T(8,128)(2,1)} %x_ref.3, bf16[8192,768]{1,0:T(8,128)(2,1)} %get-tuple-element.26.dh2_ref.r_ref, bf16[8192,3072]{1,0:T(8,128)(2,1)} %get-tuple-element.27.a1_ref, ...), custom_call_target="tpu_custom_call" | custom-call | flops 115964116992 | bytes 201326592 | tf_op jit(solution)/shard_map/k4/pallas_call | solution.py:441
  514.7 75.8 %k5.1 = (bf16[8192,768]{1,0:T(8,128)(2,1)}, f32[2,2,768,768]{3,2,1,0:T(8,128)}) custom-call(bf16[8192,3072]{1,0:T(8,128)(2,1)} %get-tuple-element.30.a_ref, bf16[768,3072]{1,0:T(8,128)(2,1)} %w_ref.3, bf16[8192,768]{1,0:T(8,128)(2,1)} %get-tuple-element.26.dh2_ref.r_ref, f32[2,768,768]{2,1,0:T(8,128)} %get-tuple-element.31.acc_in, ...), custom_call_target="tpu_custom_call" | custom-call | flops 38654705664 | bytes 75497472 | tf_op jit(solution)/shard_map/k5/pallas_call | solution.py:379
  590.6 37.0 %place.1 = (f32[768,3072]{1,0:T(8,128)}, f32[3072,768]{1,0:T(8,128)}, f32[768,3072]{1,0:T(8,128)}, f32[3072,768]{1,0:T(8,128)}, bf16[8192,768]{1,0:T(8,128)(2,1)}) custom-call(f32[2,2,768,768]{3,2,1,0:T(8,128)} %get-tuple-element.21.r2, f32[1,2,768,768]{3,2,1,0:T(8,128)} %get-tuple-element.25.r3, f32[3,2,768,768]{3,2,1,0:T(8,128)} %get-tuple-element.29.r4a.r4b, ...), custom_call_target="tpu_custom_call" | custom-call | tf_op jit(solution)/shard_map/place/pallas_call | solution.py:484

commit v4 on v3

--- a/solution.py
+++ b/solution.py
@@ -41,10 +41,9 @@
 def gelu_both(x, d):
     x2 = x * x
     t = jnp.tanh(x * (C1 + C2 * x2))
-    s = 1.0 + t
-    hx = 0.5 * x
-    w = ((1.0 - t) * s) * hx
-    return hx * s, (0.5 * s + w * (C1 + (3.0 * C2) * x2)) * d
+    cdf = 0.5 + 0.5 * t
+    h = x * cdf
+    return h, (cdf + (h * (1.0 - t)) * (C1 + (3.0 * C2) * x2)) * d
 
 
 def k1(x_ref, w1_ref, w2_ref, a1_ref, h2_ref, h1_scr, *, sub, fch):
@@ -451,8 +450,11 @@
     )(x, dh2, a1, w2, res_in)
 
 
+PQ = 2
+
+
 def place(r2, r3, r4a, r4b, r5, dx_in, dw1, dw2, dw3, dw4, dx):
-    c = pl.program_id(0) // 4
+    c = pl.program_id(0) // PQ
     dx[...] = dx_in[...]
 
     def put(cond, src, wa, wb):
@@ -469,21 +471,21 @@
 
 
 def call_place(r2, r3, r4, r5, dx):
-    rows = FC // 4
+    rows = FC // PQ
 
     def spec(lo, n, first):
         def index(t):
-            k = jnp.clip(t, 4 * lo, 4 * (lo + n) - 1)
-            return first + k // 4 - lo, 0, lax.rem(k, 4), 0
+            k = jnp.clip(t, PQ * lo, PQ * (lo + n) - 1)
+            return first + k // PQ - lo, 0, lax.rem(k, PQ), 0
 
         return pl.BlockSpec((1, 2, rows, D), index)
 
-    row = pl.BlockSpec((N // 16, D), lambda t: (t, 0))
-    wide = pl.BlockSpec((rows, FC), lambda t: (lax.rem(t, 4), t // 4))
+    row = pl.BlockSpec((N // (NC * PQ), D), lambda t: (t, 0))
+    wide = pl.BlockSpec((rows, FC), lambda t: (lax.rem(t, PQ), t // PQ))
     tall = pl.BlockSpec((rows, D), lambda t: (t, 0))
     return pl.pallas_call(
         place,
-        grid=(16,),
+        grid=(NC * PQ,),
         in_specs=[spec(0, 2, 0), spec(2, 1, 0), spec(3, 1, 0), spec(0, 2, 1), spec(2, 2, 0), row],
         out_specs=[wide, tall, wide, tall, row],
         out_shape=[jax.ShapeDtypeStruct((D, F), f32), jax.ShapeDtypeStruct((F, D), f32)] * 2 + [jax.ShapeDtypeStruct((N, D), bf)],

time: 628 us -> 612 us (0.975)
  Pallas kernels: 627 us -> 611 us
    pallas_call x1, Pallas kernels: 202 us -> 193 us  [call_k2(): pl.pallas_call(functools.partial(k2, sub=sub, ev=EV), grid=(NC, N // R),...]
where the time goes in v4:
time: 612 us
  Pallas kernels  611 us (100%)
    pallas_call x1, Pallas kernels, call_k2(): pl.pallas_call(functools.partial(k2, sub=sub, ev=EV), grid=(NC, N // R),...  193 us
    pallas_call x1, Pallas kernels, call_k4(): pl.pallas_call(functools.partial(k4, sub=sub, ev=EV4), grid=(NC, N // R),...  161 us
    pallas_call x2, Pallas kernels, call_k3(): pl.pallas_call(functools.partial(k3, sub=sub, ev=EV5 if last else EV, las...  133 us
    pallas_call x1, Pallas kernels, call_k1(): pl.pallas_call(functools.partial(k1, sub=sub, fch=fch), grid=(N // R,), i...  89 us
    pallas_call x1, Pallas kernels, call_place(): pl.pallas_call(place, grid=(NC * PQ,), in_specs=[spec(0, 2, 0), spec(2, 1...  34.2 us

profile of v4, /device:TPU:0, one launch (start us, length us, event | category | flops | bytes accessed | tf_op | source)
XLA Modules:
  0.0 611.8 jit_solution(17331381746590330745)
XLA Ops:
  0.6 89.0 %k1.1 = (bf16[8192,3072]{1,0:T(8,128)(2,1)}, bf16[8192,768]{1,0:T(8,128)(2,1)}) custom-call(bf16[8192,768]{1,0:T(8,128)(2,1)} %x_ref.3, bf16[768,3072]{1,0:T(8,128)(2,1)} %w_ref.3, bf16[3072,768]{1,0:T(8,128)(2,1)} %w2_ref.3), custom_call_target="tpu_custom_call" | custom-call | flops 77309411328 | bytes 75497472 | tf_op jit(solution)/shard_map/k1/pallas_call | solution.py:60
  89.6 193.1 %k2.1 = (bf16[8192,3072]{1,0:T(8,128)(2,1)}, f32[2,2,768,768]{3,2,1,0:T(8,128)}, f32[2,768,768]{2,1,0:T(8,128)}, f32[768,768]{1,0:T(8,128)}) custom-call(bf16[8192,768]{1,0:T(8,128)(2,1)} %get-tuple-element.20.h2_ref, bf16[8192,768]{1,0:T(8,128)(2,1)} %r_ref.1, bf16[768,3072]{1,0:T(8,128)(2,1)} %w_ref.2, bf16[3072,768]{1,0:T(8,128)(2,1)} %w4_ref.1), custom_call_target="tpu_custom_call" | custom-call | flops 154618822656 | bytes 150994944 | tf_op jit(solution)/shard_map/k2/pallas_call | solution.py:329
  282.7 57.6 %k3.1 = (bf16[8192,768]{1,0:T(8,128)(2,1)}, f32[1,2,768,768]{3,2,1,0:T(8,128)}, f32[768,768]{1,0:T(8,128)}) custom-call(bf16[8192,3072]{1,0:T(8,128)(2,1)} %get-tuple-element.22.a_ref, bf16[768,3072]{1,0:T(8,128)(2,1)} %w_ref.2, bf16[8192,768]{1,0:T(8,128)(2,1)} %r_ref.1, f32[2,768,768]{2,1,0:T(8,128)} %get-tuple-element.23.acc_in, ...), custom_call_target="tpu_custom_call" | custom-call | flops 38654705664 | bytes 75497472 | tf_op jit(solution)/shard_map/k3/pallas_call | solution.py:378
  340.3 161.4 %k4.1 = (bf16[8192,3072]{1,0:T(8,128)(2,1)}, f32[3,2,768,768]{3,2,1,0:T(8,128)}, f32[2,768,768]{2,1,0:T(8,128)}, f32[768,768]{1,0:T(8,128)}) custom-call(bf16[8192,768]{1,0:T(8,128)(2,1)} %x_ref.3, bf16[8192,768]{1,0:T(8,128)(2,1)} %get-tuple-element.26.dh2_ref.r_ref, bf16[8192,3072]{1,0:T(8,128)(2,1)} %get-tuple-element.27.a1_ref, ...), custom_call_target="tpu_custom_call" | custom-call | flops 115964116992 | bytes 201326592 | tf_op jit(solution)/shard_map/k4/pallas_call | solution.py:440
  501.8 75.9 %k5.1 = (bf16[8192,768]{1,0:T(8,128)(2,1)}, f32[2,2,768,768]{3,2,1,0:T(8,128)}) custom-call(bf16[8192,3072]{1,0:T(8,128)(2,1)} %get-tuple-element.30.a_ref, bf16[768,3072]{1,0:T(8,128)(2,1)} %w_ref.3, bf16[8192,768]{1,0:T(8,128)(2,1)} %get-tuple-element.26.dh2_ref.r_ref, f32[2,768,768]{2,1,0:T(8,128)} %get-tuple-element.31.acc_in, ...), custom_call_target="tpu_custom_call" | custom-call | flops 38654705664 | bytes 75497472 | tf_op jit(solution)/shard_map/k5/pallas_call | solution.py:378
  577.7 34.2 %place.1 = (f32[768,3072]{1,0:T(8,128)}, f32[3072,768]{1,0:T(8,128)}, f32[768,3072]{1,0:T(8,128)}, f32[3072,768]{1,0:T(8,128)}, bf16[8192,768]{1,0:T(8,128)(2,1)}) custom-call(f32[2,2,768,768]{3,2,1,0:T(8,128)} %get-tuple-element.21.r2, f32[1,2,768,768]{3,2,1,0:T(8,128)} %get-tuple-element.25.r3, f32[3,2,768,768]{3,2,1,0:T(8,128)} %get-tuple-element.29.r4a.r4b, ...), custom_call_target="tpu_custom_call" | custom-call | tf_op jit(solution)/shard_map/place/pallas_call | solution.py:486

commit v5 on v4

--- a/solution.py
+++ b/solution.py
@@ -56,7 +56,7 @@
         h2_ref[sl, :] = (nn(h1_scr[sl, :], w2_ref[...]) + x_ref[sl, :].astype(f32)).astype(bf)
 
 
-def call_k1(x, w1, w2, R=1024, sub=256, fch=768):
+def call_k1(x, w1, w2, R=1024, sub=512, fch=768):
     return pl.pallas_call(
         functools.partial(k1, sub=sub, fch=fch),
         grid=(N // R,),
@@ -253,17 +253,19 @@
         lax.fori_loop(0, n, one, 0)
 
 
-def accumulate(n, dd, ee, pp):
+def accumulate(n, dd, ee, pp, group=1):
+    done = 0
     for j in range(n):
         dd(j)
         if j > 0:
             ee(j - 1)
-        if j > 1:
-            pp(j - 2)
+        if j - 1 >= done + group:
+            pp(done // group)
+            done += group
     ee(n - 1)
-    if n > 1:
-        pp(n - 2)
-    pp(n - 1)
+    while done < n:
+        pp(done // group)
+        done += group
 
 
 def k2(h2_ref, g_ref, w3_ref, w4_ref, da3_ref, red, acc_out, res_out, a_scr, d_scr, h_scr, *scr, sub, ev):
@@ -294,11 +296,11 @@
             da3_ref[sl, :] = da.astype(bf)
 
         def pp(j):
-            sl, ss = pl.ds(r0 + j * sub, sub), pl.ds(j * sub, sub)
+            sl, ss = pl.ds(r0 + j * 2 * sub, 2 * sub), pl.ds(j * 2 * sub, 2 * sub)
             acc[slot, 1] += tn(h_scr[ss, :], g_ref[sl, :])
             acc[slot, 0] += tn(h2_ref[sl, :], da3_ref[sl, :])
 
-        accumulate(SR // sub, dd, ee, pp)
+        accumulate(SR // sub, dd, ee, pp, 2)
         comm_steps(cm, c, t, ev, acc_in=False, res_in=False, slots=2, end=True)
 
     slots_of(h2_ref.shape[0], body)

time: 612 us -> 610 us (level)
  no operation moved by 1% of the time
where the time goes in v5:
time: 610 us
  Pallas kernels  609 us (100%)
    pallas_call x1, Pallas kernels, call_k2(): pl.pallas_call(functools.partial(k2, sub=sub, ev=EV), grid=(NC, N // R),...  193 us
    pallas_call x1, Pallas kernels, call_k4(): pl.pallas_call(functools.partial(k4, sub=sub, ev=EV4), grid=(NC, N // R),...  162 us
    pallas_call x2, Pallas kernels, call_k3(): pl.pallas_call(functools.partial(k3, sub=sub, ev=EV5 if last else EV, las...  133 us
    pallas_call x1, Pallas kernels, call_k1(): pl.pallas_call(functools.partial(k1, sub=sub, fch=fch), grid=(N // R,), i...  87.1 us
    pallas_call x1, Pallas kernels, call_place(): pl.pallas_call(place, grid=(NC * PQ,), in_specs=[spec(0, 2, 0), spec(2, 1...  34.2 us

profile of v5, /device:TPU:0, one launch (start us, length us, event | category | flops | bytes accessed | tf_op | source)
XLA Modules:
  0.0 610.0 jit_solution(9390334079311390353)
XLA Ops:
  0.6 87.1 %k1.1 = (bf16[8192,3072]{1,0:T(8,128)(2,1)}, bf16[8192,768]{1,0:T(8,128)(2,1)}) custom-call(bf16[8192,768]{1,0:T(8,128)(2,1)} %x_ref.3, bf16[768,3072]{1,0:T(8,128)(2,1)} %w_ref.3, bf16[3072,768]{1,0:T(8,128)(2,1)} %w2_ref.3), custom_call_target="tpu_custom_call" | custom-call | flops 77309411328 | bytes 75497472 | tf_op jit(solution)/shard_map/k1/pallas_call | solution.py:60
  87.7 193.2 %k2.1 = (bf16[8192,3072]{1,0:T(8,128)(2,1)}, f32[2,2,768,768]{3,2,1,0:T(8,128)}, f32[2,768,768]{2,1,0:T(8,128)}, f32[768,768]{1,0:T(8,128)}) custom-call(bf16[8192,768]{1,0:T(8,128)(2,1)} %get-tuple-element.20.h2_ref, bf16[8192,768]{1,0:T(8,128)(2,1)} %r_ref.1, bf16[768,3072]{1,0:T(8,128)(2,1)} %w_ref.2, bf16[3072,768]{1,0:T(8,128)(2,1)} %w4_ref.1), custom_call_target="tpu_custom_call" | custom-call | flops 154618822656 | bytes 150994944 | tf_op jit(solution)/shard_map/k2/pallas_call | solution.py:331
  280.9 57.6 %k3.1 = (bf16[8192,768]{1,0:T(8,128)(2,1)}, f32[1,2,768,768]{3,2,1,0:T(8,128)}, f32[768,768]{1,0:T(8,128)}) custom-call(bf16[8192,3072]{1,0:T(8,128)(2,1)} %get-tuple-element.22.a_ref, bf16[768,3072]{1,0:T(8,128)(2,1)} %w_ref.2, bf16[8192,768]{1,0:T(8,128)(2,1)} %r_ref.1, f32[2,768,768]{2,1,0:T(8,128)} %get-tuple-element.23.acc_in, ...), custom_call_target="tpu_custom_call" | custom-call | flops 38654705664 | bytes 75497472 | tf_op jit(solution)/shard_map/k3/pallas_call | solution.py:380
  338.5 161.6 %k4.1 = (bf16[8192,3072]{1,0:T(8,128)(2,1)}, f32[3,2,768,768]{3,2,1,0:T(8,128)}, f32[2,768,768]{2,1,0:T(8,128)}, f32[768,768]{1,0:T(8,128)}) custom-call(bf16[8192,768]{1,0:T(8,128)(2,1)} %x_ref.3, bf16[8192,768]{1,0:T(8,128)(2,1)} %get-tuple-element.26.dh2_ref.r_ref, bf16[8192,3072]{1,0:T(8,128)(2,1)} %get-tuple-element.27.a1_ref, ...), custom_call_target="tpu_custom_call" | custom-call | flops 115964116992 | bytes 201326592 | tf_op jit(solution)/shard_map/k4/pallas_call | solution.py:442
  500.1 75.7 %k5.1 = (bf16[8192,768]{1,0:T(8,128)(2,1)}, f32[2,2,768,768]{3,2,1,0:T(8,128)}) custom-call(bf16[8192,3072]{1,0:T(8,128)(2,1)} %get-tuple-element.30.a_ref, bf16[768,3072]{1,0:T(8,128)(2,1)} %w_ref.3, bf16[8192,768]{1,0:T(8,128)(2,1)} %get-tuple-element.26.dh2_ref.r_ref, f32[2,768,768]{2,1,0:T(8,128)} %get-tuple-element.31.acc_in, ...), custom_call_target="tpu_custom_call" | custom-call | flops 38654705664 | bytes 75497472 | tf_op jit(solution)/shard_map/k5/pallas_call | solution.py:380
  575.8 34.2 %place.1 = (f32[768,3072]{1,0:T(8,128)}, f32[3072,768]{1,0:T(8,128)}, f32[768,3072]{1,0:T(8,128)}, f32[3072,768]{1,0:T(8,128)}, bf16[8192,768]{1,0:T(8,128)(2,1)}) custom-call(f32[2,2,768,768]{3,2,1,0:T(8,128)} %get-tuple-element.21.r2, f32[1,2,768,768]{3,2,1,0:T(8,128)} %get-tuple-element.25.r3, f32[3,2,768,768]{3,2,1,0:T(8,128)} %get-tuple-element.29.r4a.r4b, ...), custom_call_target="tpu_custom_call" | custom-call | tf_op jit(solution)/shard_map/place/pallas_call | solution.py:488
